TPU v7x, 1024 devices: a whole 4x8x16 slice. The times are simulated.
1024 devices in a mesh: face: 16 (over z_hi, x), tile: 16 (over y, core), lev: 4 (over z_lo).
Axes of the slice: x: 4, y: 8, z: 16 (z_hi: 4, z_lo: 4; z = z_hi * 4 + z_lo), core: 2. Of those that a mesh axis runs over, the one named last changes fastest.
Arguments:
- airflow_components: float32 [2, 72, 128, 2048], P(None, 'lev', 'face', 'tile'), may hold values from -4.5 to 4.5, as said below
- heat_state: float32 [72, 128, 2048], P('lev', 'face', 'tile'), may hold values from 0.5 to 2
- layer_pressure_depth: float32 [72, 128, 2048], P('lev', 'face', 'tile'), may hold values from 0.5 to 2
- constituent_masses: float32 [18, 72, 128, 2048], P(None, 'lev', 'face', 'tile'), may hold values from 0.1 to 1
- ground_gravity_potential: float32 [128, 2048], P('face', 'tile'), may hold values from -8 to 8
- inverse_mapping_entries: float32 [4, 128, 2048], P(None, 'face', 'tile'), may hold values from -4 to 4
- mapping_determinant: float32 [128, 2048], P('face', 'tile'), may hold values from 0.5 to 2
- interface_rightangle_rotations: int32 [16, 16, 2], replicated, may hold values from 0 to 3
- interface_flipped_markers: int32 [16, 16, 2], replicated, may hold values from 0 to 1
- corner_block_tally: int32 [16, 16], replicated, may hold values from 3 to 4
Outputs:
- airflow_next: float32 [2, 72, 128, 2048], P(None, 'lev', 'face', 'tile')
- heat_state_next: float32 [72, 128, 2048], P('lev', 'face', 'tile')
- pressure_depth_next: float32 [72, 128, 2048], P('lev', 'face', 'tile')
- constituent_masses_next: float32 [18, 72, 128, 2048], P(None, 'lev', 'face', 'tile')
- stepping_bounds: float32 [2], replicated
Inputs may be any that keep to these rules, and one draw needn't show every extreme that they name: `airflow_components`: component magnitudes grow across the grid by up to a factor of 9. `interface_rightangle_rotations`: entry [f, t, 0] concerns the boundary between blocks (f, t) and (f+1, t), entry [f, t, 1] the one between (f, t) and (f, t+1). `interface_flipped_markers`: indexed like interface_rightangle_rotations. `corner_block_tally`: entry [f, t] belongs to the corner shared by blocks (f, t), (f+1, t), (f, t+1), (f+1, t+1).
All inputs are finite; a program needn't handle non-finite values.
Results may differ from a plain program's by a relative error of at most 0.00012.
Values sent between devices are 32-bit elements; how exact they have to be, the bound alone decides.
No kernel may reach another device: no remote copies, remote signals or barrier semaphores. Data moves between devices by JAX's collectives and lax.ppermute only.
A program may use at most 32 MiB of HBM per device.

v0:
```python
import math

import jax
import jax.numpy as jnp
import numpy as np
from jax import lax
from jax.experimental import pallas as pl
from jax.experimental.pallas import tpu as pltpu
from jax.sharding import Mesh
from jax.sharding import PartitionSpec as P


FACE = ("face_0", "face_1")
TILE = ("tile_0", "tile_1")
PLANE = FACE + ("tile_0",)
COLUMN = ("tile_1", "lev")

time_step = 0.05
viscosity = 0.05

ROWS, LANES = 8, 128
VMEM = pl.BlockSpec(memory_space=pltpu.VMEM)
ANY = pl.BlockSpec(memory_space=pltpu.HBM)
SMEM = pl.BlockSpec(memory_space=pltpu.SMEM)


def gll_tables():
    offset = 1.0 / math.sqrt(5.0)
    nodes = np.array([-1.0, -offset, offset, 1.0])
    weights = np.array([1.0 / 6.0, 5.0 / 6.0, 5.0 / 6.0, 1.0 / 6.0])
    bary = np.ones(4)
    for i in range(4):
        for j in range(4):
            if j != i:
                bary[i] = bary[i] / (nodes[i] - nodes[j])
    derivative = np.zeros((4, 4))
    for i in range(4):
        for j in range(4):
            if j != i:
                derivative[i, j] = bary[j] / bary[i] / (nodes[i] - nodes[j])
        derivative[i, i] = -np.sum(derivative[i])
    return derivative, weights


DERIVATIVE, WEIGHTS = gll_tables()


def iota(axis):
    return lax.broadcasted_iota(jnp.int32, (ROWS, LANES), axis)


def by_node(place, values):
    node = place % 4
    plane = jnp.full((ROWS, LANES), float(values[0]), jnp.float32)
    for i in range(1, 4):
        plane = jnp.where(node == i, float(values[i]), plane)
    return plane


def node_weights():
    return by_node(iota(0), WEIGHTS) * by_node(iota(1), WEIGHTS)


def derivative_terms(axis, scale):
    place = iota(axis)
    terms = []
    for k in range(-3, 4):
        values = [DERIVATIVE[i, i + k] if 0 <= i + k < 4 else 0.0 for i in range(4)]
        terms.append((k, by_node(place, values) * scale))
    return terms


def derive(field, axis, terms):
    size = field.shape[axis]
    total = None
    for k, coefficient in terms:
        moved = field if k == 0 else pltpu.roll(field, (-k) % size, axis)
        part = coefficient * moved
        total = part if total is None else total + part
    return total


def tile_of(index):
    return pl.ds(pl.multiple_of(index * ROWS, ROWS), ROWS)


def beside_in_block(x, axis):
    place, size = iota(axis), x.shape[axis]
    later, earlier = pltpu.roll(x, size - 1, axis), pltpu.roll(x, 1, axis)
    before_border = (place % 4 == 3) & (place < size - 1)
    after_border = (place % 4 == 0) & (place > 0)
    return jnp.where(before_border, later, jnp.where(after_border, earlier, 0.0))


def sum_in_block(x):
    x = x + beside_in_block(x, 1)
    return x + beside_in_block(x, 0)


def lane_tables():
    swap = np.zeros((LANES, LANES))
    for c in range(3, LANES - 1, 4):
        swap[c, c + 1] = swap[c + 1, c] = 1.0
    derive_columns = np.kron(np.eye(LANES // 4), (WEIGHTS[:, None] * DERIVATIVE).T)
    full = -(derive_columns @ (np.eye(LANES) + swap)).astype(np.float32)
    high = full.astype(jnp.bfloat16)
    low = (full - high.astype(np.float32)).astype(jnp.bfloat16)
    swap = swap.astype(jnp.bfloat16)
    return np.concatenate([swap, swap, high, high, low], 0)


def halves(x):
    high = x.astype(jnp.bfloat16)
    return high, (x - high.astype(jnp.float32)).astype(jnp.bfloat16)


def pair_of(lane):
    return ((lane + 1) // 2) % (LANES // 2)


def local_kernel(
    n_share, air_in, heat_in, thick_in, tracer_in, ground_in, maps_in, det_in, table_in, w_out, packed_out, share_out,
    air, heat, thick, tracer, ground, maps, det, table, small_sem, tracer_sem,
):
    levels = heat.shape[0]
    small = [
        pltpu.make_async_copy(source, held, small_sem.at[i])
        for i, (source, held) in enumerate(
            (
                (maps_in, maps), (det_in, det), (ground_in, ground), (heat_in, heat), (thick_in, thick),
                (air_in, air), (table_in, table),
            )
        )
    ]

    def tracer_copy(level):
        return pltpu.make_async_copy(tracer_in.at[:, level], tracer.at[:, level], tracer_sem.at[level])

    for copy in small:
        copy.start()
    for level in reversed(range(levels)):
        tracer_copy(level).start()
    for copy in small:
        copy.wait()
    tracers = tracer.shape[0]
    fields = 4 + tracers
    row, lane = iota(0), iota(1)
    pair = pair_of(lane)
    row_scale = time_step * by_node(row, WEIGHTS)
    j = det[...]
    mass = j * node_weights()
    m00, m01, m10, m11 = maps[0], maps[1], maps[2], maps[3]
    j00, j01, j10, j11 = j * m00, j * m01, j * m10, j * m11
    scale = time_step * node_weights()
    undo = 1.0 / scale
    b11 = (j00 * m00 + j01 * m01) * undo
    b12 = (j00 * m10 + j01 * m11) * undo
    b22 = (j10 * m10 + j11 * m11) * undo
    along_rows = derivative_terms(0, scale)
    along_columns = derivative_terms(1, scale)
    ground_plane = ground[...]

    def one_level(level, below, speed, damp):
        u, v = air[0, level], air[1, level]
        heat_l, thick_l = heat[level], thick[level]
        term = heat_l * thick_l
        square = u * u + v * v
        energy = 0.5 * square + (ground_plane + below + 0.5 * term)
        below = below + term
        speed = jnp.maximum(speed, square)
        first, second = j00 * u + j01 * v, j10 * u + j11 * v
        second_scaled = second * row_scale

        rows, columns = derive(energy, 0, along_rows), derive(energy, 1, along_columns)
        plain = [mass * u - (j00 * rows + j10 * columns), mass * v - (j01 * rows + j11 * columns)]
        rows, columns = derive(heat_l, 0, along_rows), derive(heat_l, 1, along_columns)
        plain.append(mass * heat_l - (first * rows + second * columns))
        rows, columns = derive(thick_l, 0, along_rows), derive(thick_l, 1, along_columns)
        laplace = derive(b11 * rows + b12 * columns, 0, along_rows) + derive(b12 * rows + b22 * columns, 1, along_columns)
        damp = jnp.maximum(damp, jnp.abs(laplace))
        plain.append(mass * thick_l - derive(thick_l * first, 0, along_rows) + viscosity * laplace)
        fluxes = [thick_l * second_scaled]
        tracer_copy(level).wait()
        for t in range(tracers):
            q = tracer[t, level]
            plain.append(mass * q - derive(q * first, 0, along_rows))
            fluxes.append(q * second_scaled)
        fluxes.append(jnp.zeros_like(u))
        return below, speed, damp, plain, fluxes

    def through(plain, fluxes):
        high, low = halves(jnp.concatenate(plain, axis=0))
        swapped = jnp.dot(
            jnp.concatenate([high, low], axis=1), table[pl.ds(0, 2 * LANES), :], preferred_element_type=jnp.float32
        )
        high, low = halves(jnp.concatenate(fluxes, axis=0))
        derived = jnp.dot(
            jnp.concatenate([high, low, high], axis=1), table[pl.ds(2 * LANES, 3 * LANES), :],
            preferred_element_type=jnp.float32,
        )
        return swapped, derived

    def finish_level(level, slot, plain, swapped, derived, packed):
        for field in range(fields):
            x = plain[field] + swapped[field * ROWS : field * ROWS + ROWS]
            if field >= 3:
                x = x + derived[(field - 3) * ROWS : (field - 3) * ROWS + ROWS]
            x = x + beside_in_block(x, 0)
            w_out[tile_of(field * levels + level), :] = x
            packed = jnp.where(pair == slot + field, pltpu.roll(x, 2 * (slot + field), 1), packed)
        return packed

    summed_mass = sum_in_block(mass)
    packed_mass = pltpu.roll(summed_mass, 4 * fields, 1)

    def one(turn, carry):
        below, speed, damp = carry
        half = levels // 2 - 1 - turn
        packed = jnp.where(pair == 2 * fields, packed_mass, 0.0)
        below, speed, damp, plain_1, fluxes_1 = one_level(2 * half + 1, below, speed, damp)
        below, speed, damp, plain_0, fluxes_0 = one_level(2 * half, below, speed, damp)
        swapped, derived = through(plain_1 + plain_0, fluxes_1 + fluxes_0)
        n, m = len(plain_1) * ROWS, len(fluxes_1) * ROWS
        packed = finish_level(2 * half + 1, fields, plain_1, swapped[:n], derived[:m], packed)
        packed = finish_level(2 * half, 0, plain_0, swapped[n:], derived[m:], packed)
        packed_out[tile_of(half), :] = packed
        return below, speed, damp

    zero = jnp.zeros((ROWS, LANES), jnp.float32)
    total, speed, damp = lax.fori_loop(0, levels // 2, one, (zero, zero, zero), unroll=3)
    w_out[pl.ds(fields * levels * ROWS, ROWS), :] = summed_mass
    spare = w_out.shape[0] - (fields * levels + 1) * ROWS
    w_out[pl.ds((fields * levels + 1) * ROWS, spare), :] = jnp.zeros((spare, LANES), jnp.float32)
    spacing = jnp.sqrt(m00 * m00 + m01 * m01 + m10 * m10 + m11 * m11)
    courant = jnp.max(time_step * jnp.sqrt(speed) * spacing, axis=0, keepdims=True)
    damping = jnp.max(damp * (viscosity / mass), axis=0, keepdims=True)
    bounds = jnp.where(row == 0, courant, damping)
    for peer in range(n_share):
        share_out[peer, pl.ds(0, ROWS), :] = total
        share_out[peer, pl.ds(ROWS, ROWS), :] = bounds


def carry_kernel(levels, n_lev, shared, w, packed, maps, det, wind_out, far_out, near_out, packed_out, bound_out):
    lev, core = lax.axis_index("lev"), lax.axis_index("tile_1")
    odd = lax.rem(lax.axis_index(FACE), 2) == 1
    higher = jnp.zeros((ROWS, LANES), jnp.float32)
    bounds = shared[0, pl.ds(ROWS, ROWS), :]
    for peer in range(shared.shape[0]):
        counts = (peer // n_lev == core) & (peer % n_lev > lev)
        higher = higher + jnp.where(counts, shared[peer, pl.ds(0, ROWS), :], 0.0)
        bounds = jnp.maximum(bounds, shared[peer, pl.ds(ROWS, ROWS), :])
    lane = iota(1)
    pair = pair_of(lane)
    both = jnp.maximum(bounds, pltpu.roll(bounds, LANES // 2, 1))
    line = jnp.where(lane[0:1] < LANES // 2, both[0:1], both[1:2])
    bound_out[...] = jnp.broadcast_to(line[None], bound_out.shape)

    scale = time_step * node_weights()
    j = det[...]
    rows = derive(higher, 0, derivative_terms(0, scale))
    columns = derive(higher, 1, derivative_terms(1, scale))
    add_u = sum_in_block(-j * (maps[0] * rows + maps[2] * columns))
    add_v = sum_in_block(-j * (maps[1] * rows + maps[3] * columns))
    for field, add in ((0, add_u), (1, add_v)):
        for level in range(levels):
            at = pl.ds((field * levels + level) * ROWS, ROWS)
            wind_out[at, :] = w[at, :] + add
    halves_of_levels = packed.shape[0] // ROWS
    corner_rows = 2 * ROWS
    edge_rows = far_out.shape[0] - corner_rows
    for start in range(0, edge_rows, ROWS):
        last = w[pl.ds(start * ROWS + ROWS - 1, ROWS, stride=ROWS), :]
        first = w[pl.ds(start * ROWS, ROWS, stride=ROWS), :]
        far_out[pl.ds(start, ROWS), :] = jnp.where(odd, last, first)
        near_out[pl.ds(start, ROWS), :] = jnp.where(odd, first, last)
    for out, ends in ((far_out, odd), (near_out, jnp.logical_not(odd))):
        for start, add in ((0, add_u), (levels, add_v)):
            at = pl.ds(start, levels)
            out[at, :] = out[at, :] + jnp.where(ends, add[ROWS - 1 : ROWS], add[0:1])
        out[pl.ds(edge_rows, corner_rows), :] = jnp.zeros((corner_rows, LANES), jnp.float32)
    n_fields = (w.shape[0] // ROWS - 1) // levels
    add = jnp.zeros((ROWS, LANES), jnp.float32)
    for slot in (0, n_fields):
        add = jnp.where(pair == slot, pltpu.roll(add_u, 2 * slot, 1), add)
        add = jnp.where(pair == slot + 1, pltpu.roll(add_v, 2 * slot + 2, 1), add)
    for half in range(halves_of_levels):
        at = pl.ds(half * ROWS, ROWS)
        x = packed[at, :] + add
        packed_out[at, :] = x
        for out, ends in ((far_out, odd), (near_out, jnp.logical_not(odd))):
            out[pl.ds(edge_rows + half, 1), :] = jnp.where(ends, x[ROWS - 1 : ROWS], x[0:1])


def cosine_sine(code):
    cosine = jnp.where(code == 0, 1.0, jnp.where(code == 2, -1.0, 0.0)).astype(jnp.float32)
    sine = jnp.where(code == 1, 1.0, jnp.where(code == 3, -1.0, 0.0)).astype(jnp.float32)
    return cosine, sine


def turned(u, v, code):
    cosine, sine = cosine_sine(code)
    return cosine * u - sine * v, sine * u + cosine * v


def sum_kernel(
    levels, n_face, n_tile, rotations, flips, valences, w, wind, far, near, inside, outside,
    air_out, heat_out, thick_out, tracer_out, up_rim, down_rim, side_rim,
    air_held, heat_held, thick_held, tracer_held, out_sem,
):
    face, tile = lax.axis_index(FACE), lax.axis_index(TILE)
    face_lower = lax.rem(face + n_face - 1, n_face)
    tile_lower = lax.rem(tile + n_tile - 1, n_tile)

    def at(f, t):
        return f * n_tile + t

    top_code = (4 - rotations[2 * at(face_lower, tile)]) & 3
    bottom_code = rotations[2 * at(face, tile)]
    west_code = (4 - rotations[2 * at(face, tile_lower) + 1]) & 3
    east_code = rotations[2 * at(face, tile) + 1]
    top_flip = flips[2 * at(face_lower, tile)]
    bottom_flip = flips[2 * at(face, tile)]
    west_flip = flips[2 * at(face, tile_lower) + 1]
    east_flip = flips[2 * at(face, tile) + 1]
    corners = {
        ("up", "west"): valences[at(face_lower, tile_lower)],
        ("up", "east"): valences[at(face_lower, tile)],
        ("down", "west"): valences[at(face, tile_lower)],
        ("down", "east"): valences[at(face, tile)],
    }
    row, lane = iota(0), iota(1)
    pair = pair_of(lane)
    tracers = tracer_out.shape[0]
    fields = 4 + tracers
    count = side_rim.shape[0]

    edge_rows = up_rim.shape[0]
    odd_face, odd_tile = lax.rem(face, 2) == 1, lax.rem(tile, 2) == 1
    for out, flag, by_near in ((up_rim, top_flip, odd_face), (down_rim, bottom_flip, jnp.logical_not(odd_face))):
        places = jnp.where(flag == 1, LANES - 1 - lane, lane)
        for start in range(0, edge_rows, ROWS):
            rows = pl.ds(start, ROWS)
            x = jnp.where(by_near, near[rows, :], far[rows, :])
            out[rows, :] = jnp.take_along_axis(x, places, axis=1, mode="promise_in_bounds")

    within = jnp.where(pair >= fields, pair - fields, pair)
    is_u, is_v = (within == 0) & (pair < 2 * fields), within == 1

    def turn_packed(x, code):
        cosine, sine = cosine_sine(code)
        rows = x.shape[0]
        u, v = (jnp.broadcast_to(mask[0:1], (rows, LANES)) for mask in (is_u.astype(jnp.int32), is_v.astype(jnp.int32)))
        from_v, from_u = pltpu.roll(x, LANES - 2, 1), pltpu.roll(x, 2, 1)
        return jnp.where(u == 1, cosine * x - sine * from_v, jnp.where(v == 1, sine * from_u + cosine * x, x))

    def side(from_inside, flag, code, name):
        def rows_at(start, rows):
            at = pl.ds(start, rows)
            return jnp.where(from_inside, inside[at, :], outside[at, :])

        far_end, near_end = rows_at(count * ROWS, 2 * ROWS), rows_at((count + 2) * ROWS, 2 * ROWS)
        ends = []
        for end, row_code, by_near in (("up", top_code, odd_face), ("down", bottom_code, jnp.logical_not(odd_face))):
            corner = turn_packed(jnp.where(by_near, near_end, far_end), (row_code + code) & 3)
            ends.append(jnp.where(corners[end, name] == 4, corner, 0.0))
        columns = []
        for half in range(count):
            start = half * ROWS
            x = jnp.concatenate(
                [rows_at(start + jnp.where(flag == 1, ROWS - 1 - r, r), 1) for r in range(ROWS)], axis=0
            )
            x = turn_packed(x, code)
            over = [jnp.broadcast_to(end[half : half + 1], (ROWS, LANES)) for end in ends]
            columns.append(x + jnp.where(row == 0, over[0], jnp.where(row == ROWS - 1, over[1], 0.0)))
        return columns

    wests = side(odd_tile, west_flip, west_code, "west")
    easts = side(jnp.logical_not(odd_tile), east_flip, east_code, "east")
    for half in range(count):
        side_rim[half] = jnp.where(lane % 2 == 0, pltpu.roll(wests[half], 1, 1), pltpu.roll(easts[half], LANES - 1, 1))

    at_side = (lane == 0) | (lane == LANES - 1)

    def summed(x, upper, lower, sides, slot):
        x = x + jnp.where(row == 0, upper, jnp.where(row == ROWS - 1, lower, 0.0))
        moved = pltpu.roll(sides, (LANES - 2 * slot) % LANES, 1) if slot else sides
        return x + jnp.where(at_side, moved, 0.0)

    def rim(ref, index):
        return jnp.broadcast_to(ref[pl.ds(index, 1), :], (ROWS, LANES))

    index = fields * levels
    mass = summed(w[pl.ds(index * ROWS, ROWS), :], rim(up_rim, index), rim(down_rim, index), side_rim[0], 2 * fields)
    scale = 1.0 / mass

    def one(half, _):
        sides = side_rim[half]
        for part in range(2):
            level, slot = 2 * half + part, part * fields
            u_at, v_at = level, levels + level
            upper = turned(rim(up_rim, u_at), rim(up_rim, v_at), top_code)
            lower = turned(rim(down_rim, u_at), rim(down_rim, v_at), bottom_code)
            air_held[0, level] = summed(wind[tile_of(u_at), :], upper[0], lower[0], sides, slot) * scale
            air_held[1, level] = summed(wind[tile_of(v_at), :], upper[1], lower[1], sides, slot + 1) * scale
            for field in range(2, fields):
                index = field * levels + level
                x = w[tile_of(index), :]
                x = summed(x, rim(up_rim, index), rim(down_rim, index), sides, slot + field) * scale
                if field == 2:
                    heat_held[level] = x
                elif field == 3:
                    thick_held[level] = x
                else:
                    tracer_held[field - 4, level] = x
            for copy in copies_out(level):
                copy.start()
        return 0

    def copies_out(level):
        return (
            pltpu.make_async_copy(air_held.at[:, level], air_out.at[:, level], out_sem.at[0, level]),
            pltpu.make_async_copy(heat_held.at[level], heat_out.at[level], out_sem.at[1, level]),
            pltpu.make_async_copy(thick_held.at[level], thick_out.at[level], out_sem.at[2, level]),
            pltpu.make_async_copy(tracer_held.at[:, level], tracer_out.at[:, level], out_sem.at[3, level]),
        )

    def finish(level, _):
        for copy in copies_out(level):
            copy.wait()
        return 0

    lax.fori_loop(0, levels // 2, one, 0)
    lax.fori_loop(0, levels, finish, 0)


def swap_pairs(x, axes, start):
    count = lax.axis_size(axes)
    pairs = [(i % count, (i + 1) % count) for i in range(start, count + start, 2)]
    return lax.ppermute(x, axes, pairs + [(j, i) for i, j in pairs])


def bounds_kernel(plane, out):
    both = jnp.max(plane[...], axis=0)
    lane = lax.broadcasted_iota(jnp.int32, (1, LANES), 1)
    for i in range(2):
        out[i] = jnp.max(jnp.where(lane // (LANES // 2) == i, both, 0.0))


def on_device(air, heat, thick, tracer, ground, maps, det, rotations, flips, valences):
    levels = heat.shape[0]
    tracers = tracer.shape[0]
    fields = 4 + tracers
    edge_rows = -(-(fields * levels + 1) // ROWS) * ROWS
    count = levels // 2
    n_lev = lax.axis_size("lev")
    n_share = lax.axis_size(COLUMN)
    n_face, n_tile = lax.axis_size(FACE), lax.axis_size(TILE)
    n_plane = lax.axis_size(PLANE)

    def f32(*shape):
        return jax.ShapeDtypeStruct(shape, jnp.float32)

    inputs = (air, heat, thick, tracer, ground, maps, det, jnp.asarray(lane_tables()))
    inputs = tuple(pltpu.with_memory_space_constraint(x, pltpu.HBM) for x in inputs)
    params = pltpu.CompilerParams(vmem_limit_bytes=24 * 1024 * 1024)
    w, packed, share = pl.pallas_call(
        lambda *refs: local_kernel(n_share, *refs),
        out_shape=(f32(edge_rows * ROWS, LANES), f32(count * ROWS, LANES), f32(n_share, 2 * ROWS, LANES)),
        in_specs=[ANY] * 8,
        out_specs=(VMEM,) * 3,
        scratch_shapes=[pltpu.VMEM(x.shape, x.dtype) for x in inputs]
        + [pltpu.SemaphoreType.DMA((7,)), pltpu.SemaphoreType.DMA((levels,))],
        compiler_params=params,
        name="local",
    )(*inputs)
    shared = lax.all_to_all(share, COLUMN, 0, 0, tiled=True)
    wind, far, near, packed, bound = pl.pallas_call(
        lambda *refs: carry_kernel(levels, n_lev, *refs),
        out_shape=(
            f32(2 * levels * ROWS, LANES),
            f32(edge_rows + 2 * ROWS, LANES),
            f32(edge_rows + 2 * ROWS, LANES),
            f32(count * ROWS, LANES),
            f32(n_plane, 1, LANES),
        ),
        in_specs=[VMEM] * 5,
        out_specs=(VMEM,) * 5,
        compiler_params=params,
        name="carry",
    )(shared, w, packed, maps, det)
    far = swap_pairs(far, FACE, 1)
    near = swap_pairs(near, FACE, 0)
    plane = lax.all_to_all(bound, PLANE, 0, 0, tiled=True)
    stepping_bounds = pl.pallas_call(
        bounds_kernel, out_shape=f32(2), in_specs=[VMEM], out_specs=SMEM, compiler_params=params, name="bounds"
    )(plane)
    sides = jnp.concatenate([packed, far[edge_rows:], near[edge_rows:]], 0)
    inside = swap_pairs(sides, TILE, 0)
    outside = swap_pairs(sides, TILE, 1)
    sums = pl.pallas_call(
        lambda *refs: sum_kernel(levels, n_face, n_tile, *refs),
        out_shape=(f32(*air.shape), f32(*heat.shape), f32(*thick.shape), f32(*tracer.shape)),
        in_specs=[SMEM] * 3 + [VMEM] * 6,
        out_specs=(ANY,) * 4,
        scratch_shapes=[
            pltpu.VMEM((edge_rows, LANES), jnp.float32),
            pltpu.VMEM((edge_rows, LANES), jnp.float32),
            pltpu.VMEM((count, ROWS, LANES), jnp.float32),
            *(pltpu.VMEM(x.shape, jnp.float32) for x in (air, heat, thick, tracer)),
            pltpu.SemaphoreType.DMA((4, levels)),
        ],
        compiler_params=params,
        name="sum",
    )
    air_next, heat_next, thick_next, tracer_next = sums(rotations.reshape(-1), flips.reshape(-1), valences.reshape(-1), w, wind, far, near, inside, outside)
    return air_next, heat_next, thick_next, tracer_next, stepping_bounds


def solution(mesh):
    face, tile, lev = mesh.shape["face"], mesh.shape["tile"], mesh.shape["lev"]
    inner = min(face, 4)
    split = Mesh(
        mesh.devices.reshape(face // inner, inner, tile // 2, 2, lev),
        ("face_0", "face_1", "tile_0", "tile_1", "lev"),
    )
    level_plane = P("lev", FACE, TILE)
    field_level_plane = P(None, "lev", FACE, TILE)
    return jax.shard_map(
        on_device,
        mesh=split,
        in_specs=(
            field_level_plane, level_plane, level_plane, field_level_plane,
            P(FACE, TILE), P(None, FACE, TILE), P(FACE, TILE), P(), P(), P(),
        ),
        out_specs=(field_level_plane, level_plane, level_plane, field_level_plane, P()),
        check_vma=False,
    )
```

profile of v0, /device:TPU:6, one launch (start us, length us, event | category | flops | bytes accessed | tf_op | source)
XLA Modules:
  0.0 78.5 jit_solution(12519740665139858004)
XLA Ops:
  0.6 0.0 copy-start.1
  0.6 0.0 copy-start
  0.7 7.3 %local.1 = (f32[3200,128]{1,0:T(8,128)S(1)}, f32[72,128]{1,0:T(8,128)S(1)}, f32[8,16,128]{2,1,0:T(8,128)S(1)}) custom-call(f32[2,18,8,128]{3,2,1,0:T(8,128)} %refs_0_.1, f32[18,8,128]{2,1,0:T(8,128)} %refs_1_.1, f32[18,8,128]{2,1,0:T(8,128)} %refs_2_.1, f32[18,18,8,128]{3,2,1,0:T(8,128)} %refs_3_.2, f32[8,128]{1,0:T(8,128)} %refs_4_.2, ...), custom_call_target="tpu_custom_call" | custom-call | tf_op jit(solution)/shard_map/local/pallas_call | solution.py:466
  8.0 0.0 copy-start.4
  8.0 0.0 copy-start.2
  8.0 0.0 copy-start.3
  8.0 13.2 %all_to_all.10.refs_0_ = f32[8,16,128]{2,1,0:T(8,128)S(1)} all-to-all(f32[8,16,128]{2,1,0:T(8,128)S(1)} %get-tuple-element.18), channel_id=1, replica_groups=mesh['face_0'=4,'face_1'=4,'tile_0'=8,'tile_1'=2,'lev'=4] {'tile_1','lev'}, dimensions={0} | all-to-all | bytes 131072 | tf_op jit(solution)/shard_map/all_to_all | solution.py:476
  21.2 0.0 copy-done.1
  21.2 0.0 copy-done
  21.2 0.9 %carry.1 = (f32[288,128]{1,0:T(8,128)S(1)}, f32[416,128]{1,0:T(8,128)S(1)}, f32[416,128]{1,0:T(8,128)S(1)}, f32[72,128]{1,0:T(8,128)S(1)}, f32[128,1,128]{2,1,0:T(1,128)}) custom-call(f32[8,16,128]{2,1,0:T(8,128)S(1)} %all_to_all.10.refs_0_, f32[3200,128]{1,0:T(8,128)S(1)} %get-tuple-element.17.refs_1_.refs_3_, f32[72,128]{1,0:T(8,128)S(1)} %get-tuple-element.19.refs_2_, ...), custom_call_target="tpu_custom_call" | custom-call | tf_op jit(solution)/shard_map/carry/pallas_call | solution.py:477
  22.1 10.8 %collective-permute-start = (f32[416,128]{1,0:T(8,128)S(1)}, f32[416,128]{1,0:T(8,128)S(1)}, u32[]{:S(2)}, u32[]{:S(2)}) collective-permute-start(f32[416,128]{1,0:T(8,128)S(1)} %get-tuple-element.21), channel_id=1, source_target_pairs={{64,128},{192,256},{320,384},{448,512},{576,640},{704,768},{832,89... | collective-permute-start | bytes 638984 | tf_op jit(solution)/shard_map/ppermute | solution.py:439
  33.0 1.9 %collective-permute-start.1 = (f32[416,128]{1,0:T(8,128)S(1)}, f32[416,128]{1,0:T(8,128)S(1)}, u32[]{:S(2)}, u32[]{:S(2)}) collective-permute-start(f32[416,128]{1,0:T(8,128)S(1)} %get-tuple-element.22), channel_id=1, source_target_pairs={{0,64},{128,192},{256,320},{384,448},{512,576},{640,704},{768,832}... | collective-permute-start | bytes 638984 | tf_op jit(solution)/shard_map/ppermute | solution.py:439
  34.9 22.0 %all-to-all-start.1 = ((f32[128,1,128]{2,1,0:T(1,128)}), f32[128,1,128]{2,1,0:T(1,128)S(1)}, u32[]{:S(2)}, u32[]{:S(2)}) async-start(f32[128,1,128]{2,1,0:T(1,128)} %get-tuple-element.28), calls=%async_computation.1 | async-start | bytes 131072 | tf_op jit(solution)/shard_map/all_to_all | solution.py:493
  56.9 0.0 collective-permute-done.refs_5_
  56.9 0.0 collective-permute-done.1.refs_6_
  57.0 3.2 %collective-permute-start.3 = (f32[104,128]{1,0:T(8,128)S(1)}, f32[104,128]{1,0:T(8,128)S(1)}, u32[]{:S(2)}, u32[]{:S(2)}) collective-permute-start(f32[104,128]{1,0:T(8,128)S(1)} %pad_maximum_fusion), channel_id=1, source_target_pairs={{4,8},{12,16},{20,24},{28,32},{36,40},{44,48},{52,56},{60,0},{8,4}... | collective-permute-start | bytes 159752 | tf_op jit(solution)/shard_map/ppermute | solution.py:439
  60.2 2.2 %collective-permute-start.2 = (f32[104,128]{1,0:T(8,128)S(1)}, f32[104,128]{1,0:T(8,128)S(1)}, u32[]{:S(2)}, u32[]{:S(2)}) collective-permute-start(f32[104,128]{1,0:T(8,128)S(1)} %pad_maximum_fusion), channel_id=1, source_target_pairs={{0,4},{8,12},{16,20},{24,28},{32,36},{40,44},{48,52},{56,60},{4,0}... | collective-permute-start | bytes 159752 | tf_op jit(solution)/shard_map/ppermute | solution.py:439
  62.4 0.0 copy-done.4
  62.4 0.1 reshape.21.refs_2_
  62.5 0.0 copy-done.2
  62.5 0.2 copy.16
  62.6 0.1 reshape.19.refs_0_
  62.8 0.0 copy-done.3
  62.8 0.2 copy.17
  63.0 0.1 reshape.20.refs_1_
  63.1 11.4 %all-to-all-done.1.plane = f32[128,1,128]{2,1,0:T(1,128)S(1)} async-done(((f32[128,1,128]{2,1,0:T(1,128)}), f32[128,1,128]{2,1,0:T(1,128)S(1)}, u32[]{:S(2)}, u32[]{:S(2)}) %all-to-all-start.1) | async-done | bytes 65568 | tf_op jit(solution)/shard_map/all_to_all | solution.py:493
  74.5 0.7 bounds.1
  75.2 0.0 collective-permute-done.3.refs_8_
  75.2 0.0 collective-permute-done.2.refs_7_
  75.2 3.4 %sum.1 = (f32[2,18,8,128]{3,2,1,0:T(8,128)}, f32[18,8,128]{2,1,0:T(8,128)}, f32[18,8,128]{2,1,0:T(8,128)}, f32[18,18,8,128]{3,2,1,0:T(8,128)}) custom-call(s32[512]{0:T(512)S(1)} %reshape.19.refs_0_, s32[512]{0:T(512)S(1)} %reshape.20.refs_1_, s32[256]{0:T(256)S(1)} %reshape.21.refs_2_, f32[3200,128]{1,0:T(8,128)S(1)} %get-tuple-element.17.refs_1_.refs_3_, ...), custom_call_target="tpu_custom_call" | custom-call | tf_op jit(solution)/shard_map/sum/pallas_call | solution.py:515
  (3 shorter events, 0.0 us)
Async XLA Ops:
  0.6 20.6 %copy-start.1 = (f32[8,128]{1,0:T(8,128)S(1)}, f32[8,128]{1,0:T(8,128)}, u32[]{:S(2)}) copy-start(f32[8,128]{1,0:T(8,128)} %refs_4_.3) | copy-start | bytes 12292
  0.6 20.6 %copy-start = (f32[4,8,128]{2,1,0:T(8,128)S(1)}, f32[4,8,128]{2,1,0:T(8,128)}, u32[]{:S(2)}) copy-start(f32[4,8,128]{2,1,0:T(8,128)} %refs_3_.3) | copy-start | bytes 49156
  8.0 54.4 %copy-start.4 = (s32[16,16]{1,0:T(8,128)S(1)}, s32[16,16]{1,0:T(8,128)}, u32[]{:S(2)}) copy-start(s32[16,16]{1,0:T(8,128)} %param.20) | copy-start | bytes 3076
  8.0 54.5 %copy-start.2 = (s32[16,16,2]{1,2,0:T(2,128)S(1)}, s32[16,16,2]{1,2,0:T(2,128)}, u32[]{:S(2)}) copy-start(s32[16,16,2]{1,2,0:T(2,128)} %param.18) | copy-start | bytes 6148
  8.0 54.8 %copy-start.3 = (s32[16,16,2]{1,2,0:T(2,128)S(1)}, s32[16,16,2]{1,2,0:T(2,128)}, u32[]{:S(2)}) copy-start(s32[16,16,2]{1,2,0:T(2,128)} %param.19) | copy-start | bytes 6148
  22.1 34.8 %collective-permute-start = (f32[416,128]{1,0:T(8,128)S(1)}, f32[416,128]{1,0:T(8,128)S(1)}, u32[]{:S(2)}, u32[]{:S(2)}) collective-permute-start(f32[416,128]{1,0:T(8,128)S(1)} %get-tuple-element.21), channel_id=1, source_target_pairs={{64,128},{192,256},{320,384},{448,512},{576,640},{704,768},{832,89... | collective-permute-start | bytes 638984 | tf_op jit(solution)/shard_map/ppermute | solution.py:439
  33.0 24.0 %collective-permute-start.1 = (f32[416,128]{1,0:T(8,128)S(1)}, f32[416,128]{1,0:T(8,128)S(1)}, u32[]{:S(2)}, u32[]{:S(2)}) collective-permute-start(f32[416,128]{1,0:T(8,128)S(1)} %get-tuple-element.22), channel_id=1, source_target_pairs={{0,64},{128,192},{256,320},{384,448},{512,576},{640,704},{768,832}... | collective-permute-start | bytes 638984 | tf_op jit(solution)/shard_map/ppermute | solution.py:439
  34.9 39.6 %all-to-all-start.1 = ((f32[128,1,128]{2,1,0:T(1,128)}), f32[128,1,128]{2,1,0:T(1,128)S(1)}, u32[]{:S(2)}, u32[]{:S(2)}) async-start(f32[128,1,128]{2,1,0:T(1,128)} %get-tuple-element.28), calls=%async_computation.1 | async-start | bytes 131072 | tf_op jit(solution)/shard_map/all_to_all | solution.py:493
  57.0 18.2 %collective-permute-start.3 = (f32[104,128]{1,0:T(8,128)S(1)}, f32[104,128]{1,0:T(8,128)S(1)}, u32[]{:S(2)}, u32[]{:S(2)}) collective-permute-start(f32[104,128]{1,0:T(8,128)S(1)} %pad_maximum_fusion), channel_id=1, source_target_pairs={{4,8},{12,16},{20,24},{28,32},{36,40},{44,48},{52,56},{60,0},{8,4}... | collective-permute-start | bytes 159752 | tf_op jit(solution)/shard_map/ppermute | solution.py:439
  60.2 15.0 %collective-permute-start.2 = (f32[104,128]{1,0:T(8,128)S(1)}, f32[104,128]{1,0:T(8,128)S(1)}, u32[]{:S(2)}, u32[]{:S(2)}) collective-permute-start(f32[104,128]{1,0:T(8,128)S(1)} %pad_maximum_fusion), channel_id=1, source_target_pairs={{0,4},{8,12},{16,20},{24,28},{32,36},{40,44},{48,52},{56,60},{4,0}... | collective-permute-start | bytes 159752 | tf_op jit(solution)/shard_map/ppermute | solution.py:439
where the time goes:
time: 79.3 us; the launch traced here: 78.5 us
  starting transfers between devices  40.1 us (51%)
  blocking collectives  13.2 us (17%)
  Pallas kernels  12.3 us (16%)
  waiting for transfers between devices  11.4 us (14%)
  between operations  0.81 us (1%)
    all_to_all x1, starting transfers between devices, on_device(): plane = lax.all_to_all(bound, PLANE, 0, 0, tiled=True)  22 us
    ppermute x4, starting transfers between devices, swap_pairs(): return lax.ppermute(x, axes, pairs + [(j, i) for i, j in pairs])  18.1 us
    all_to_all x1, blocking collectives, on_device(): shared = lax.all_to_all(share, COLUMN, 0, 0, tiled=True)  13.2 us
    all_to_all x1, waiting for transfers between devices, on_device(): plane = lax.all_to_all(bound, PLANE, 0, 0, tiled=True)  11.4 us
    pallas_call x1, Pallas kernels, on_device(): pl.pallas_call(lambda *refs: local_kernel(n_share, *refs), out_shape=(f32...  7.31 us
    pallas_call x1, Pallas kernels, on_device(): sums(rotations.reshape(-1), flips.reshape(-1), valences.reshape(-1), w, w...  3.36 us
  transfers between devices with their start and end apart: 5, of which 1 were waited for; matrix products, arithmetic and copies ran while one was open for 1% of the time, Pallas kernels for 1%

commit v1 on v0

--- a/solution.py
+++ b/solution.py
@@ -118,39 +118,34 @@
     return ((lane + 1) // 2) % (LANES // 2)
 
 
-def local_kernel(
-    n_share, air_in, heat_in, thick_in, tracer_in, ground_in, maps_in, det_in, table_in, w_out, packed_out, share_out,
-    air, heat, thick, tracer, ground, maps, det, table, small_sem, tracer_sem,
+def planes(maps, det):
+    j = det[...]
+    m00, m01, m10, m11 = maps[0], maps[1], maps[2], maps[3]
+    return j, j * node_weights(), (m00, m01, m10, m11), (j * m00, j * m01, j * m10, j * m11)
+
+
+def dynamics_kernel(
+    n_share, n_fields, air_in, heat_in, thick_in, ground_in, maps_in, det_in, table_in, tracer_in,
+    w_out, packed_out, share_out, first_out, second_out, mass_out, table_out, tracer_out,
+    air, heat, thick, ground, maps, det, sems,
 ):
     levels = heat.shape[0]
-    small = [
-        pltpu.make_async_copy(source, held, small_sem.at[i])
+    copies = [
+        pltpu.make_async_copy(source, held, sems.at[i])
         for i, (source, held) in enumerate(
             (
-                (maps_in, maps), (det_in, det), (ground_in, ground), (heat_in, heat), (thick_in, thick),
-                (air_in, air), (table_in, table),
+                (maps_in, maps), (det_in, det), (ground_in, ground), (heat_in, heat), (thick_in, thick), (air_in, air),
+                (table_in, table_out), (tracer_in, tracer_out),
             )
         )
     ]
-
-    def tracer_copy(level):
-        return pltpu.make_async_copy(tracer_in.at[:, level], tracer.at[:, level], tracer_sem.at[level])
-
-    for copy in small:
+    for copy in copies:
         copy.start()
-    for level in reversed(range(levels)):
-        tracer_copy(level).start()
-    for copy in small:
+    for copy in copies[:-2]:
         copy.wait()
-    tracers = tracer.shape[0]
-    fields = 4 + tracers
     row, lane = iota(0), iota(1)
     pair = pair_of(lane)
-    row_scale = time_step * by_node(row, WEIGHTS)
-    j = det[...]
-    mass = j * node_weights()
-    m00, m01, m10, m11 = maps[0], maps[1], maps[2], maps[3]
-    j00, j01, j10, j11 = j * m00, j * m01, j * m10, j * m11
+    j, mass, (m00, m01, m10, m11), (j00, j01, j10, j11) = planes(maps, det)
     scale = time_step * node_weights()
     undo = 1.0 / scale
     b11 = (j00 * m00 + j01 * m01) * undo
@@ -159,8 +154,12 @@
     along_rows = derivative_terms(0, scale)
     along_columns = derivative_terms(1, scale)
     ground_plane = ground[...]
-
-    def one_level(level, below, speed, damp):
+    row_scale = time_step * by_node(row, WEIGHTS)
+
+    def flux(first, second):
+        return derive(first, 0, along_rows) + derive(second, 1, along_columns)
+
+    def one_level(level, slot, below, speed, damp, packed):
         u, v = air[0, level], air[1, level]
         heat_l, thick_l = heat[level], thick[level]
         term = heat_l * thick_l
@@ -169,26 +168,62 @@
         below = below + term
         speed = jnp.maximum(speed, square)
         first, second = j00 * u + j01 * v, j10 * u + j11 * v
-        second_scaled = second * row_scale
-
+        first_out[level] = first
+        second_out[level] = second * row_scale
         rows, columns = derive(energy, 0, along_rows), derive(energy, 1, along_columns)
-        plain = [mass * u - (j00 * rows + j10 * columns), mass * v - (j01 * rows + j11 * columns)]
+        new = [mass * u - (j00 * rows + j10 * columns), mass * v - (j01 * rows + j11 * columns)]
         rows, columns = derive(heat_l, 0, along_rows), derive(heat_l, 1, along_columns)
-        plain.append(mass * heat_l - (first * rows + second * columns))
+        new.append(mass * heat_l - (first * rows + second * columns))
         rows, columns = derive(thick_l, 0, along_rows), derive(thick_l, 1, along_columns)
-        laplace = derive(b11 * rows + b12 * columns, 0, along_rows) + derive(b12 * rows + b22 * columns, 1, along_columns)
+        laplace = flux(b11 * rows + b12 * columns, b12 * rows + b22 * columns)
         damp = jnp.maximum(damp, jnp.abs(laplace))
-        plain.append(mass * thick_l - derive(thick_l * first, 0, along_rows) + viscosity * laplace)
-        fluxes = [thick_l * second_scaled]
-        tracer_copy(level).wait()
-        for t in range(tracers):
-            q = tracer[t, level]
-            plain.append(mass * q - derive(q * first, 0, along_rows))
-            fluxes.append(q * second_scaled)
-        fluxes.append(jnp.zeros_like(u))
-        return below, speed, damp, plain, fluxes
-
-    def through(plain, fluxes):
+        new.append(mass * thick_l - flux(thick_l * first, thick_l * second) + viscosity * laplace)
+        for field, x in enumerate(new):
+            x = sum_in_block(x)
+            w_out[tile_of(field * levels + level), :] = x
+            packed = jnp.where(pair == slot + field, pltpu.roll(x, 2 * (slot + field), 1), packed)
+        return below, speed, damp, packed
+
+    packed_mass = pltpu.roll(sum_in_block(mass), 4 * n_fields, 1)
+
+    def one(turn, carry):
+        half = levels // 2 - 1 - turn
+        packed = jnp.where(pair == 2 * n_fields, packed_mass, 0.0)
+        *carry, packed = one_level(2 * half + 1, n_fields, *carry, packed)
+        *carry, packed = one_level(2 * half, 0, *carry, packed)
+        packed_out[tile_of(half), :] = packed
+        return tuple(carry)
+
+    zero = jnp.zeros((ROWS, LANES), jnp.float32)
+    total, speed, damp = lax.fori_loop(0, levels // 2, one, (zero, zero, zero), unroll=3)
+    spacing = jnp.sqrt(m00 * m00 + m01 * m01 + m10 * m10 + m11 * m11)
+    courant = jnp.max(time_step * jnp.sqrt(speed) * spacing, axis=0, keepdims=True)
+    damping = jnp.max(damp * (viscosity / mass), axis=0, keepdims=True)
+    bounds = jnp.where(row == 0, courant, damping)
+    for peer in range(n_share):
+        share_out[peer, pl.ds(0, ROWS), :] = total
+        share_out[peer, pl.ds(ROWS, ROWS), :] = bounds
+    mass_out[...] = mass
+    for copy in copies[-2:]:
+        copy.wait()
+
+
+def tracer_kernel(firsts, seconds, mass_in, table, tracer, before, w_out, packed_out):
+    tracers, levels = tracer.shape[:2]
+    n_fields = 4 + tracers
+    pair = pair_of(iota(1))
+    mass = mass_in[...]
+    along_rows = derivative_terms(0, time_step * node_weights())
+
+    def one(half, _):
+        packed = before[tile_of(half), :]
+        plain, fluxes = [], []
+        for level in (2 * half, 2 * half + 1):
+            first, second = firsts[level], seconds[level]
+            for t in range(tracers):
+                q = tracer[t, level]
+                plain.append(mass * q - derive(q * first, 0, along_rows))
+                fluxes.append(q * second)
         high, low = halves(jnp.concatenate(plain, axis=0))
         swapped = jnp.dot(
             jnp.concatenate([high, low], axis=1), table[pl.ds(0, 2 * LANES), :], preferred_element_type=jnp.float32
@@ -198,49 +233,25 @@
             jnp.concatenate([high, low, high], axis=1), table[pl.ds(2 * LANES, 3 * LANES), :],
             preferred_element_type=jnp.float32,
         )
-        return swapped, derived
-
-    def finish_level(level, slot, plain, swapped, derived, packed):
-        for field in range(fields):
-            x = plain[field] + swapped[field * ROWS : field * ROWS + ROWS]
-            if field >= 3:
-                x = x + derived[(field - 3) * ROWS : (field - 3) * ROWS + ROWS]
+        for i, x in enumerate(plain):
+            part, t = i // tracers, i % tracers
+            at = slice(i * ROWS, i * ROWS + ROWS)
+            x = x + swapped[at] + derived[at]
             x = x + beside_in_block(x, 0)
-            w_out[tile_of(field * levels + level), :] = x
-            packed = jnp.where(pair == slot + field, pltpu.roll(x, 2 * (slot + field), 1), packed)
-        return packed
-
-    summed_mass = sum_in_block(mass)
-    packed_mass = pltpu.roll(summed_mass, 4 * fields, 1)
-
-    def one(turn, carry):
-        below, speed, damp = carry
-        half = levels // 2 - 1 - turn
-        packed = jnp.where(pair == 2 * fields, packed_mass, 0.0)
-        below, speed, damp, plain_1, fluxes_1 = one_level(2 * half + 1, below, speed, damp)
-        below, speed, damp, plain_0, fluxes_0 = one_level(2 * half, below, speed, damp)
-        swapped, derived = through(plain_1 + plain_0, fluxes_1 + fluxes_0)
-        n, m = len(plain_1) * ROWS, len(fluxes_1) * ROWS
-        packed = finish_level(2 * half + 1, fields, plain_1, swapped[:n], derived[:m], packed)
-        packed = finish_level(2 * half, 0, plain_0, swapped[n:], derived[m:], packed)
+            w_out[tile_of(t * levels + 2 * half + part), :] = x
+            slot = part * n_fields + 4 + t
+            packed = jnp.where(pair == slot, pltpu.roll(x, 2 * slot, 1), packed)
         packed_out[tile_of(half), :] = packed
-        return below, speed, damp
-
-    zero = jnp.zeros((ROWS, LANES), jnp.float32)
-    total, speed, damp = lax.fori_loop(0, levels // 2, one, (zero, zero, zero), unroll=3)
-    w_out[pl.ds(fields * levels * ROWS, ROWS), :] = summed_mass
-    spare = w_out.shape[0] - (fields * levels + 1) * ROWS
-    w_out[pl.ds((fields * levels + 1) * ROWS, spare), :] = jnp.zeros((spare, LANES), jnp.float32)
-    spacing = jnp.sqrt(m00 * m00 + m01 * m01 + m10 * m10 + m11 * m11)
-    courant = jnp.max(time_step * jnp.sqrt(speed) * spacing, axis=0, keepdims=True)
-    damping = jnp.max(damp * (viscosity / mass), axis=0, keepdims=True)
-    bounds = jnp.where(row == 0, courant, damping)
-    for peer in range(n_share):
-        share_out[peer, pl.ds(0, ROWS), :] = total
-        share_out[peer, pl.ds(ROWS, ROWS), :] = bounds
-
-
-def carry_kernel(levels, n_lev, shared, w, packed, maps, det, wind_out, far_out, near_out, packed_out, bound_out):
+        return 0
+
+    lax.fori_loop(0, levels // 2, one, 0, unroll=3)
+    tiles = tracers * levels
+    w_out[pl.ds(tiles * ROWS, ROWS), :] = sum_in_block(mass)
+    spare = w_out.shape[0] - (tiles + 1) * ROWS
+    w_out[pl.ds((tiles + 1) * ROWS, spare), :] = jnp.zeros((spare, LANES), jnp.float32)
+
+
+def carry_kernel(levels, n_lev, shared, dynamics, w, packed, maps, det, wind_out, far_out, near_out, packed_out, bound_out):
     lev, core = lax.axis_index("lev"), lax.axis_index("tile_1")
     odd = lax.rem(lax.axis_index(FACE), 2) == 1
     higher = jnp.zeros((ROWS, LANES), jnp.float32)
@@ -264,13 +275,15 @@
     for field, add in ((0, add_u), (1, add_v)):
         for level in range(levels):
             at = pl.ds((field * levels + level) * ROWS, ROWS)
-            wind_out[at, :] = w[at, :] + add
+            wind_out[at, :] = dynamics[at, :] + add
     halves_of_levels = packed.shape[0] // ROWS
     corner_rows = 2 * ROWS
     edge_rows = far_out.shape[0] - corner_rows
+    held = 4 * levels
     for start in range(0, edge_rows, ROWS):
-        last = w[pl.ds(start * ROWS + ROWS - 1, ROWS, stride=ROWS), :]
-        first = w[pl.ds(start * ROWS, ROWS, stride=ROWS), :]
+        source, place = (dynamics, start * ROWS) if start < held else (w, (start - held) * ROWS)
+        last = source[pl.ds(place + ROWS - 1, ROWS, stride=ROWS), :]
+        first = source[pl.ds(place, ROWS, stride=ROWS), :]
         far_out[pl.ds(start, ROWS), :] = jnp.where(odd, last, first)
         near_out[pl.ds(start, ROWS), :] = jnp.where(odd, first, last)
     for out, ends in ((far_out, odd), (near_out, jnp.logical_not(odd))):
@@ -278,7 +291,7 @@
             at = pl.ds(start, levels)
             out[at, :] = out[at, :] + jnp.where(ends, add[ROWS - 1 : ROWS], add[0:1])
         out[pl.ds(edge_rows, corner_rows), :] = jnp.zeros((corner_rows, LANES), jnp.float32)
-    n_fields = (w.shape[0] // ROWS - 1) // levels
+    n_fields = 4 + (w.shape[0] // ROWS - 1) // levels
     add = jnp.zeros((ROWS, LANES), jnp.float32)
     for slot in (0, n_fields):
         add = jnp.where(pair == slot, pltpu.roll(add_u, 2 * slot, 1), add)
@@ -303,7 +316,7 @@
 
 
 def sum_kernel(
-    levels, n_face, n_tile, rotations, flips, valences, w, wind, far, near, inside, outside,
+    levels, n_face, n_tile, rotations, flips, valences, w, dynamics, wind, far, near, inside, outside,
     air_out, heat_out, thick_out, tracer_out, up_rim, down_rim, side_rim,
     air_held, heat_held, thick_held, tracer_held, out_sem,
 ):
@@ -390,7 +403,7 @@
         return jnp.broadcast_to(ref[pl.ds(index, 1), :], (ROWS, LANES))
 
     index = fields * levels
-    mass = summed(w[pl.ds(index * ROWS, ROWS), :], rim(up_rim, index), rim(down_rim, index), side_rim[0], 2 * fields)
+    mass = summed(w[pl.ds((index - 4 * levels) * ROWS, ROWS), :], rim(up_rim, index), rim(down_rim, index), side_rim[0], 2 * fields)
     scale = 1.0 / mass
 
     def one(half, _):
@@ -404,7 +417,7 @@
             air_held[1, level] = summed(wind[tile_of(v_at), :], upper[1], lower[1], sides, slot + 1) * scale
             for field in range(2, fields):
                 index = field * levels + level
-                x = w[tile_of(index), :]
+                x = dynamics[tile_of(index), :] if field < 4 else w[tile_of(index - 4 * levels), :]
                 x = summed(x, rim(up_rim, index), rim(down_rim, index), sides, slot + field) * scale
                 if field == 2:
                     heat_held[level] = x
@@ -460,20 +473,38 @@
     def f32(*shape):
         return jax.ShapeDtypeStruct(shape, jnp.float32)
 
-    inputs = (air, heat, thick, tracer, ground, maps, det, jnp.asarray(lane_tables()))
-    inputs = tuple(pltpu.with_memory_space_constraint(x, pltpu.HBM) for x in inputs)
+    def in_hbm(x):
+        return pltpu.with_memory_space_constraint(x, pltpu.HBM)
+
+    inputs = tuple(in_hbm(x) for x in (air, heat, thick, ground, maps, det, jnp.asarray(lane_tables()), tracer))
     params = pltpu.CompilerParams(vmem_limit_bytes=24 * 1024 * 1024)
-    w, packed, share = pl.pallas_call(
-        lambda *refs: local_kernel(n_share, *refs),
-        out_shape=(f32(edge_rows * ROWS, LANES), f32(count * ROWS, LANES), f32(n_share, 2 * ROWS, LANES)),
+    dynamics, packed, share, *for_tracers = pl.pallas_call(
+        lambda *refs: dynamics_kernel(n_share, fields, *refs),
+        out_shape=(
+            f32(4 * levels * ROWS, LANES),
+            f32(count * ROWS, LANES),
+            f32(n_share, 2 * ROWS, LANES),
+            f32(levels, ROWS, LANES),
+            f32(levels, ROWS, LANES),
+            f32(ROWS, LANES),
+            jax.ShapeDtypeStruct(inputs[6].shape, inputs[6].dtype),
+            f32(*tracer.shape),
+        ),
         in_specs=[ANY] * 8,
-        out_specs=(VMEM,) * 3,
-        scratch_shapes=[pltpu.VMEM(x.shape, x.dtype) for x in inputs]
-        + [pltpu.SemaphoreType.DMA((7,)), pltpu.SemaphoreType.DMA((levels,))],
+        out_specs=(VMEM,) * 8,
+        scratch_shapes=[pltpu.VMEM(x.shape, x.dtype) for x in inputs[:6]] + [pltpu.SemaphoreType.DMA((8,))],
         compiler_params=params,
-        name="local",
+        name="dynamics",
     )(*inputs)
     shared = lax.all_to_all(share, COLUMN, 0, 0, tiled=True)
+    w, packed = pl.pallas_call(
+        tracer_kernel,
+        out_shape=(f32((edge_rows - 4 * levels) * ROWS, LANES), f32(count * ROWS, LANES)),
+        in_specs=[VMEM] * 6,
+        out_specs=(VMEM,) * 2,
+        compiler_params=params,
+        name="tracers",
+    )(*for_tracers, packed)
     wind, far, near, packed, bound = pl.pallas_call(
         lambda *refs: carry_kernel(levels, n_lev, *refs),
         out_shape=(
@@ -483,11 +514,11 @@
             f32(count * ROWS, LANES),
             f32(n_plane, 1, LANES),
         ),
-        in_specs=[VMEM] * 5,
+        in_specs=[VMEM] * 6,
         out_specs=(VMEM,) * 5,
         compiler_params=params,
         name="carry",
-    )(shared, w, packed, maps, det)
+    )(shared, dynamics, w, packed, maps, det)
     far = swap_pairs(far, FACE, 1)
     near = swap_pairs(near, FACE, 0)
     plane = lax.all_to_all(bound, PLANE, 0, 0, tiled=True)
@@ -500,7 +531,7 @@
     sums = pl.pallas_call(
         lambda *refs: sum_kernel(levels, n_face, n_tile, *refs),
         out_shape=(f32(*air.shape), f32(*heat.shape), f32(*thick.shape), f32(*tracer.shape)),
-        in_specs=[SMEM] * 3 + [VMEM] * 6,
+        in_specs=[SMEM] * 3 + [VMEM] * 7,
         out_specs=(ANY,) * 4,
         scratch_shapes=[
             pltpu.VMEM((edge_rows, LANES), jnp.float32),
@@ -512,7 +543,7 @@
         compiler_params=params,
         name="sum",
     )
-    air_next, heat_next, thick_next, tracer_next = sums(rotations.reshape(-1), flips.reshape(-1), valences.reshape(-1), w, wind, far, near, inside, outside)
+    air_next, heat_next, thick_next, tracer_next = sums(rotations.reshape(-1), flips.reshape(-1), valences.reshape(-1), w, dynamics, wind, far, near, inside, outside)
     return air_next, heat_next, thick_next, tracer_next, stepping_bounds
 
 

time: 79.3 us -> 75.6 us (0.953)
  blocking collectives: 13.2 us -> 0 us
  starting transfers between devices: 40.1 us -> 47.4 us
  waiting for transfers between devices: 11.4 us -> 15 us
  Pallas kernels: 12.3 us -> 10.8 us
    all_to_all x1 -> x0, blocking collectives: 13.2 us -> none  [on_device(): shared = lax.all_to_all(share, COLUMN, 0, 0, tiled=True)]
    all_to_all x0 -> x1, starting transfers between devices: none -> 7.28 us  [on_device(): shared = lax.all_to_all(share, COLUMN, 0, 0, tiled=True)]
    all_to_all x0 -> x1, waiting for transfers between devices: none -> 3.66 us  [on_device(): shared = lax.all_to_all(share, COLUMN, 0, 0, tiled=True)]
    pallas_call x2 -> x3, Pallas kernels: 10.7 us -> 9.18 us  [the longest x1 3.51 us: on_device(): pl.pallas_call(lambda *refs: dynamics_kernel(n_share, fields, *refs), out...]
  transfers between devices with their start and end apart: 5 -> 6, of which waited for: 1 -> 2; matrix products, arithmetic and copies ran while one was open for 1% -> 1% of each run, Pallas kernels for 1% -> 4%
where the time goes in v1:
time: 75.6 us; the launch traced here: 74.8 us
  starting transfers between devices  47.4 us (63%)
  waiting for transfers between devices  15 us (20%)
  Pallas kernels  10.8 us (14%)
  between operations  0.81 us (1%)
    all_to_all x1, starting transfers between devices, on_device(): plane = lax.all_to_all(bound, PLANE, 0, 0, tiled=True)  22 us
    ppermute x4, starting transfers between devices, swap_pairs(): return lax.ppermute(x, axes, pairs + [(j, i) for i, j in pairs])  18.1 us
    all_to_all x1, waiting for transfers between devices, on_device(): plane = lax.all_to_all(bound, PLANE, 0, 0, tiled=True)  11.4 us
    all_to_all x1, starting transfers between devices, on_device(): shared = lax.all_to_all(share, COLUMN, 0, 0, tiled=True)  7.28 us
    all_to_all x1, waiting for transfers between devices, on_device(): shared = lax.all_to_all(share, COLUMN, 0, 0, tiled=True)  3.66 us
    pallas_call x1, Pallas kernels, on_device(): pl.pallas_call(lambda *refs: dynamics_kernel(n_share, fields, *refs), out...  3.51 us
    pallas_call x1, Pallas kernels, on_device(): sums(rotations.reshape(-1), flips.reshape(-1), valences.reshape(-1), w, d...  3.36 us
    pallas_call x1, Pallas kernels, on_device(): pl.pallas_call(tracer_kernel, out_shape=(f32((edge_rows - 4 * levels) * R...  2.31 us
  transfers between devices with their start and end apart: 6, of which 2 were waited for; matrix products, arithmetic and copies ran while one was open for 1% of the time, Pallas kernels for 4%

profile of v1, /device:TPU:6, one launch (start us, length us, event | category | flops | bytes accessed | tf_op | source)
XLA Modules:
  0.0 74.8 jit_solution(16511325436578383211)
XLA Ops:
  0.6 3.5 %dynamics.1 = (f32[576,128]{1,0:T(8,128)S(1)}, f32[72,128]{1,0:T(8,128)S(1)}, f32[8,16,128]{2,1,0:T(8,128)}, f32[18,8,128]{2,1,0:T(8,128)S(1)}, f32[18,8,128]{2,...) custom-call(f32[2,18,8,128]{3,2,1,0:T(8,128)} %refs_0_.1, ...), custom_call_target="tpu_custom_call" | custom-call | tf_op jit(solution)/shard_map/dynamics/pallas_call | solution.py:481
  4.2 0.0 copy-start
  4.2 0.0 copy-start.1
  4.2 7.3 %all-to-all-start = ((f32[8,16,128]{2,1,0:T(8,128)}), f32[8,16,128]{2,1,0:T(8,128)S(1)}, u32[]{:S(2)}, u32[]{:S(2)}) async-start(f32[8,16,128]{2,1,0:T(8,128)} %get-tuple-element.32), calls=%async_computation | async-start | bytes 131072 | tf_op jit(solution)/shard_map/all_to_all | solution.py:499
  11.5 2.3 %tracers.1 = (f32[2624,128]{1,0:T(8,128)S(1)}, f32[72,128]{1,0:T(8,128)S(1)}) custom-call(f32[18,8,128]{2,1,0:T(8,128)S(1)} %get-tuple-element.24.firsts, f32[18,8,128]{2,1,0:T(8,128)S(1)} %get-tuple-element.25.seconds, f32[8,128]{1,0:T(8,128)S(1)} %get-tuple-element.26.mass_in, bf16[640,128]{1,0:T(8,128)(2,1)S(1)} %get-tuple-element.27.table, ...), custom_call_target="tpu_custom_call" | custom-call | tf_op jit(solution)/shard_map/tracers/pallas_call | solution.py:500
  13.8 0.0 copy-start.4
  13.8 0.0 copy-start.2
  13.8 0.0 copy-start.3
  13.8 3.7 %all-to-all-done.refs_0_ = f32[8,16,128]{2,1,0:T(8,128)S(1)} async-done(((f32[8,16,128]{2,1,0:T(8,128)}), f32[8,16,128]{2,1,0:T(8,128)S(1)}, u32[]{:S(2)}, u32[]{:S(2)}) %all-to-all-start) | async-done | bytes 65568 | tf_op jit(solution)/shard_map/all_to_all | solution.py:499
  17.5 0.0 copy-done
  17.5 0.0 copy-done.1
  17.5 0.9 %carry.1 = (f32[288,128]{1,0:T(8,128)S(1)}, f32[416,128]{1,0:T(8,128)S(1)}, f32[416,128]{1,0:T(8,128)S(1)}, f32[72,128]{1,0:T(8,128)S(1)}, f32[128,1,128]{2,1,0:T(1,128)}) custom-call(f32[8,16,128]{2,1,0:T(8,128)S(1)} %all-to-all-done.refs_0_, f32[576,128]{1,0:T(8,128)S(1)} %get-tuple-element.31.refs_1_.refs_4_, ...), custom_call_target="tpu_custom_call" | custom-call | tf_op jit(solution)/shard_map/carry/pallas_call | solution.py:508
  18.4 10.8 %collective-permute-start = (f32[416,128]{1,0:T(8,128)S(1)}, f32[416,128]{1,0:T(8,128)S(1)}, u32[]{:S(2)}, u32[]{:S(2)}) collective-permute-start(f32[416,128]{1,0:T(8,128)S(1)} %get-tuple-element.35), channel_id=1, source_target_pairs={{64,128},{192,256},{320,384},{448,512},{576,640},{704,768},{832,89... | collective-permute-start | bytes 638984 | tf_op jit(solution)/shard_map/ppermute | solution.py:452
  29.2 1.9 %collective-permute-start.1 = (f32[416,128]{1,0:T(8,128)S(1)}, f32[416,128]{1,0:T(8,128)S(1)}, u32[]{:S(2)}, u32[]{:S(2)}) collective-permute-start(f32[416,128]{1,0:T(8,128)S(1)} %get-tuple-element.36), channel_id=1, source_target_pairs={{0,64},{128,192},{256,320},{384,448},{512,576},{640,704},{768,832}... | collective-permute-start | bytes 638984 | tf_op jit(solution)/shard_map/ppermute | solution.py:452
  31.1 22.0 %all-to-all-start.1 = ((f32[128,1,128]{2,1,0:T(1,128)}), f32[128,1,128]{2,1,0:T(1,128)S(1)}, u32[]{:S(2)}, u32[]{:S(2)}) async-start(f32[128,1,128]{2,1,0:T(1,128)} %get-tuple-element.42), calls=%async_computation.1 | async-start | bytes 131072 | tf_op jit(solution)/shard_map/all_to_all | solution.py:524
  53.2 0.0 collective-permute-done.refs_6_
  53.2 0.0 collective-permute-done.1.refs_7_
  53.2 3.2 %collective-permute-start.3 = (f32[104,128]{1,0:T(8,128)S(1)}, f32[104,128]{1,0:T(8,128)S(1)}, u32[]{:S(2)}, u32[]{:S(2)}) collective-permute-start(f32[104,128]{1,0:T(8,128)S(1)} %pad_maximum_fusion), channel_id=1, source_target_pairs={{4,8},{12,16},{20,24},{28,32},{36,40},{44,48},{52,56},{60,0},{8,4}... | collective-permute-start | bytes 159752 | tf_op jit(solution)/shard_map/ppermute | solution.py:452
  56.4 2.2 %collective-permute-start.2 = (f32[104,128]{1,0:T(8,128)S(1)}, f32[104,128]{1,0:T(8,128)S(1)}, u32[]{:S(2)}, u32[]{:S(2)}) collective-permute-start(f32[104,128]{1,0:T(8,128)S(1)} %pad_maximum_fusion), channel_id=1, source_target_pairs={{0,4},{8,12},{16,20},{24,28},{32,36},{40,44},{48,52},{56,60},{4,0}... | collective-permute-start | bytes 159752 | tf_op jit(solution)/shard_map/ppermute | solution.py:452
  58.6 0.0 copy-done.4
  58.6 0.1 reshape.21.refs_2_
  58.7 0.0 copy-done.2
  58.7 0.2 copy.16
  58.9 0.1 reshape.19.refs_0_
  59.0 0.0 copy-done.3
  59.0 0.2 copy.17
  59.2 0.1 reshape.20.refs_1_
  59.4 11.4 %all-to-all-done.1.plane = f32[128,1,128]{2,1,0:T(1,128)S(1)} async-done(((f32[128,1,128]{2,1,0:T(1,128)}), f32[128,1,128]{2,1,0:T(1,128)S(1)}, u32[]{:S(2)}, u32[]{:S(2)}) %all-to-all-start.1) | async-done | bytes 65568 | tf_op jit(solution)/shard_map/all_to_all | solution.py:524
  70.7 0.7 bounds.1
  71.4 0.0 collective-permute-done.3.refs_9_
  71.4 0.0 collective-permute-done.2.refs_8_
  71.4 3.4 %sum.1 = (f32[2,18,8,128]{3,2,1,0:T(8,128)}, f32[18,8,128]{2,1,0:T(8,128)}, f32[18,8,128]{2,1,0:T(8,128)}, f32[18,18,8,128]{3,2,1,0:T(8,128)}) custom-call(s32[512]{0:T(512)S(1)} %reshape.19.refs_0_, s32[512]{0:T(512)S(1)} %reshape.20.refs_1_, s32[256]{0:T(256)S(1)} %reshape.21.refs_2_, f32[2624,128]{1,0:T(8,128)S(1)} %get-tuple-element.30.refs_2_.refs_3_, ...), custom_call_target="tpu_custom_call" | custom-call | tf_op jit(solution)/shard_map/sum/pallas_call | solution.py:546
  (3 shorter events, 0.0 us)
Async XLA Ops:
  4.2 13.3 %copy-start = (f32[4,8,128]{2,1,0:T(8,128)S(1)}, f32[4,8,128]{2,1,0:T(8,128)}, u32[]{:S(2)}) copy-start(f32[4,8,128]{2,1,0:T(8,128)} %refs_4_.3) | copy-start | bytes 49156
  4.2 13.3 %copy-start.1 = (f32[8,128]{1,0:T(8,128)S(1)}, f32[8,128]{1,0:T(8,128)}, u32[]{:S(2)}) copy-start(f32[8,128]{1,0:T(8,128)} %refs_5_.3) | copy-start | bytes 12292
  4.2 13.3 %all-to-all-start = ((f32[8,16,128]{2,1,0:T(8,128)}), f32[8,16,128]{2,1,0:T(8,128)S(1)}, u32[]{:S(2)}, u32[]{:S(2)}) async-start(f32[8,16,128]{2,1,0:T(8,128)} %get-tuple-element.32), calls=%async_computation | async-start | bytes 131072 | tf_op jit(solution)/shard_map/all_to_all | solution.py:499
  13.8 44.9 %copy-start.4 = (s32[16,16]{1,0:T(8,128)S(1)}, s32[16,16]{1,0:T(8,128)}, u32[]{:S(2)}) copy-start(s32[16,16]{1,0:T(8,128)} %param.20) | copy-start | bytes 3076
  13.8 44.9 %copy-start.2 = (s32[16,16,2]{1,2,0:T(2,128)S(1)}, s32[16,16,2]{1,2,0:T(2,128)}, u32[]{:S(2)}) copy-start(s32[16,16,2]{1,2,0:T(2,128)} %param.18) | copy-start | bytes 6148
  13.8 45.3 %copy-start.3 = (s32[16,16,2]{1,2,0:T(2,128)S(1)}, s32[16,16,2]{1,2,0:T(2,128)}, u32[]{:S(2)}) copy-start(s32[16,16,2]{1,2,0:T(2,128)} %param.19) | copy-start | bytes 6148
  18.4 34.8 %collective-permute-start = (f32[416,128]{1,0:T(8,128)S(1)}, f32[416,128]{1,0:T(8,128)S(1)}, u32[]{:S(2)}, u32[]{:S(2)}) collective-permute-start(f32[416,128]{1,0:T(8,128)S(1)} %get-tuple-element.35), channel_id=1, source_target_pairs={{64,128},{192,256},{320,384},{448,512},{576,640},{704,768},{832,89... | collective-permute-start | bytes 638984 | tf_op jit(solution)/shard_map/ppermute | solution.py:452
  29.2 24.0 %collective-permute-start.1 = (f32[416,128]{1,0:T(8,128)S(1)}, f32[416,128]{1,0:T(8,128)S(1)}, u32[]{:S(2)}, u32[]{:S(2)}) collective-permute-start(f32[416,128]{1,0:T(8,128)S(1)} %get-tuple-element.36), channel_id=1, source_target_pairs={{0,64},{128,192},{256,320},{384,448},{512,576},{640,704},{768,832}... | collective-permute-start | bytes 638984 | tf_op jit(solution)/shard_map/ppermute | solution.py:452
  31.1 39.6 %all-to-all-start.1 = ((f32[128,1,128]{2,1,0:T(1,128)}), f32[128,1,128]{2,1,0:T(1,128)S(1)}, u32[]{:S(2)}, u32[]{:S(2)}) async-start(f32[128,1,128]{2,1,0:T(1,128)} %get-tuple-element.42), calls=%async_computation.1 | async-start | bytes 131072 | tf_op jit(solution)/shard_map/all_to_all | solution.py:524
  53.2 18.2 %collective-permute-start.3 = (f32[104,128]{1,0:T(8,128)S(1)}, f32[104,128]{1,0:T(8,128)S(1)}, u32[]{:S(2)}, u32[]{:S(2)}) collective-permute-start(f32[104,128]{1,0:T(8,128)S(1)} %pad_maximum_fusion), channel_id=1, source_target_pairs={{4,8},{12,16},{20,24},{28,32},{36,40},{44,48},{52,56},{60,0},{8,4}... | collective-permute-start | bytes 159752 | tf_op jit(solution)/shard_map/ppermute | solution.py:452
  56.4 15.0 %collective-permute-start.2 = (f32[104,128]{1,0:T(8,128)S(1)}, f32[104,128]{1,0:T(8,128)S(1)}, u32[]{:S(2)}, u32[]{:S(2)}) collective-permute-start(f32[104,128]{1,0:T(8,128)S(1)} %pad_maximum_fusion), channel_id=1, source_target_pairs={{0,4},{8,12},{16,20},{24,28},{32,36},{40,44},{48,52},{56,60},{4,0}... | collective-permute-start | bytes 159752 | tf_op jit(solution)/shard_map/ppermute | solution.py:452

commit v2 on v1

--- a/solution.py
+++ b/solution.py
@@ -124,18 +124,18 @@
     return j, j * node_weights(), (m00, m01, m10, m11), (j * m00, j * m01, j * m10, j * m11)
 
 
-def dynamics_kernel(
-    n_share, n_fields, air_in, heat_in, thick_in, ground_in, maps_in, det_in, table_in, tracer_in,
-    w_out, packed_out, share_out, first_out, second_out, mass_out, table_out, tracer_out,
-    air, heat, thick, ground, maps, det, sems,
-):
-    levels = heat.shape[0]
+def column_kernel(n_share, *refs):
+    air_in, heat_in, thick_in, ground_in, maps_in, det_in, table_in = refs[:7]
+    share_out, levels_out, planes_out, table, sems = refs[7:]
+    levels = levels_out.shape[1]
+    air, heat, thick = levels_out.at[pl.ds(3, 2)], levels_out.at[5], levels_out.at[6]
+    maps, det, ground = planes_out.at[pl.ds(0, 4)], planes_out.at[4], planes_out.at[5]
     copies = [
         pltpu.make_async_copy(source, held, sems.at[i])
         for i, (source, held) in enumerate(
             (
-                (maps_in, maps), (det_in, det), (ground_in, ground), (heat_in, heat), (thick_in, thick), (air_in, air),
-                (table_in, table_out), (tracer_in, tracer_out),
+                (maps_in, maps), (det_in, det), (thick_in, thick), (heat_in, heat), (air_in, air),
+                (ground_in, ground), (table_in, table),
             )
         )
     ]
@@ -143,9 +143,8 @@
         copy.start()
     for copy in copies[:-2]:
         copy.wait()
-    row, lane = iota(0), iota(1)
-    pair = pair_of(lane)
-    j, mass, (m00, m01, m10, m11), (j00, j01, j10, j11) = planes(maps, det)
+    row = iota(0)
+    _, mass, (m00, m01, m10, m11), (j00, j01, j10, j11) = planes(maps, det)
     scale = time_step * node_weights()
     undo = 1.0 / scale
     b11 = (j00 * m00 + j01 * m01) * undo
@@ -153,49 +152,22 @@
     b22 = (j10 * m10 + j11 * m11) * undo
     along_rows = derivative_terms(0, scale)
     along_columns = derivative_terms(1, scale)
-    ground_plane = ground[...]
     row_scale = time_step * by_node(row, WEIGHTS)
 
-    def flux(first, second):
-        return derive(first, 0, along_rows) + derive(second, 1, along_columns)
-
-    def one_level(level, slot, below, speed, damp, packed):
-        u, v = air[0, level], air[1, level]
-        heat_l, thick_l = heat[level], thick[level]
-        term = heat_l * thick_l
-        square = u * u + v * v
-        energy = 0.5 * square + (ground_plane + below + 0.5 * term)
-        below = below + term
-        speed = jnp.maximum(speed, square)
-        first, second = j00 * u + j01 * v, j10 * u + j11 * v
-        first_out[level] = first
-        second_out[level] = second * row_scale
-        rows, columns = derive(energy, 0, along_rows), derive(energy, 1, along_columns)
-        new = [mass * u - (j00 * rows + j10 * columns), mass * v - (j01 * rows + j11 * columns)]
-        rows, columns = derive(heat_l, 0, along_rows), derive(heat_l, 1, along_columns)
-        new.append(mass * heat_l - (first * rows + second * columns))
+    def one(level, carry):
+        total, speed, damp = carry
+        u, v, thick_l = air[0, level], air[1, level], thick[level]
+        total = total + heat[level] * thick_l
+        speed = jnp.maximum(speed, u * u + v * v)
+        levels_out[0, level] = j00 * u + j01 * v
+        levels_out[1, level] = (j10 * u + j11 * v) * row_scale
         rows, columns = derive(thick_l, 0, along_rows), derive(thick_l, 1, along_columns)
-        laplace = flux(b11 * rows + b12 * columns, b12 * rows + b22 * columns)
-        damp = jnp.maximum(damp, jnp.abs(laplace))
-        new.append(mass * thick_l - flux(thick_l * first, thick_l * second) + viscosity * laplace)
-        for field, x in enumerate(new):
-            x = sum_in_block(x)
-            w_out[tile_of(field * levels + level), :] = x
-            packed = jnp.where(pair == slot + field, pltpu.roll(x, 2 * (slot + field), 1), packed)
-        return below, speed, damp, packed
-
-    packed_mass = pltpu.roll(sum_in_block(mass), 4 * n_fields, 1)
-
-    def one(turn, carry):
-        half = levels // 2 - 1 - turn
-        packed = jnp.where(pair == 2 * n_fields, packed_mass, 0.0)
-        *carry, packed = one_level(2 * half + 1, n_fields, *carry, packed)
-        *carry, packed = one_level(2 * half, 0, *carry, packed)
-        packed_out[tile_of(half), :] = packed
-        return tuple(carry)
+        laplace = derive(b11 * rows + b12 * columns, 0, along_rows) + derive(b12 * rows + b22 * columns, 1, along_columns)
+        levels_out[2, level] = laplace
+        return total, speed, jnp.maximum(damp, jnp.abs(laplace))
 
     zero = jnp.zeros((ROWS, LANES), jnp.float32)
-    total, speed, damp = lax.fori_loop(0, levels // 2, one, (zero, zero, zero), unroll=3)
+    total, speed, damp = lax.fori_loop(0, levels, one, (zero, zero, zero), unroll=6)
     spacing = jnp.sqrt(m00 * m00 + m01 * m01 + m10 * m10 + m11 * m11)
     courant = jnp.max(time_step * jnp.sqrt(speed) * spacing, axis=0, keepdims=True)
     damping = jnp.max(damp * (viscosity / mass), axis=0, keepdims=True)
@@ -203,16 +175,70 @@
     for peer in range(n_share):
         share_out[peer, pl.ds(0, ROWS), :] = total
         share_out[peer, pl.ds(ROWS, ROWS), :] = bounds
-    mass_out[...] = mass
+    planes_out[6] = mass
     for copy in copies[-2:]:
         copy.wait()
 
 
-def tracer_kernel(firsts, seconds, mass_in, table, tracer, before, w_out, packed_out):
+def fields_kernel(by_level, by_point, table, tracer_in, dynamics_out, w_out, packed_out, tracer, sem):
+    copy = pltpu.make_async_copy(tracer_in, tracer, sem.at[0])
+    copy.start()
+    firsts, seconds, laplaces = by_level.at[0], by_level.at[1], by_level.at[2]
+    air, heat, thick = by_level.at[pl.ds(3, 2)], by_level.at[5], by_level.at[6]
+    maps, det, ground = by_point.at[pl.ds(0, 4)], by_point.at[4], by_point.at[5]
+    dynamics(firsts, laplaces, air, heat, thick, ground, maps, det, tracer, dynamics_out, packed_out)
+    copy.wait()
+    tracers_of(firsts, seconds, by_point[6], table, tracer, packed_out, w_out, packed_out)
+
+
+def dynamics(firsts, laplaces, air, heat, thick, ground, maps, det, tracer, w_out, packed_out):
+    levels = heat.shape[0]
+    n_fields = 4 + tracer.shape[0]
+    lane = iota(1)
+    pair = pair_of(lane)
+    _, mass, _, (j00, j01, j10, j11) = planes(maps, det)
+    scale = time_step * node_weights()
+    along_rows = derivative_terms(0, scale)
+    along_columns = derivative_terms(1, scale)
+    ground_plane = ground[...]
+
+    def flux(first, second):
+        return derive(first, 0, along_rows) + derive(second, 1, along_columns)
+
+    def one_level(level, slot, below, packed):
+        u, v = air[0, level], air[1, level]
+        heat_l, thick_l = heat[level], thick[level]
+        term = heat_l * thick_l
+        energy = 0.5 * (u * u + v * v) + (ground_plane + below + 0.5 * term)
+        first, second = firsts[level], j10 * u + j11 * v
+        rows, columns = derive(energy, 0, along_rows), derive(energy, 1, along_columns)
+        new = [mass * u - (j00 * rows + j10 * columns), mass * v - (j01 * rows + j11 * columns)]
+        rows, columns = derive(heat_l, 0, along_rows), derive(heat_l, 1, along_columns)
+        new.append(mass * heat_l - (first * rows + second * columns))
+        new.append(mass * thick_l - flux(thick_l * first, thick_l * second) + viscosity * laplaces[level])
+        for field, x in enumerate(new):
+            x = sum_in_block(x)
+            w_out[tile_of(field * levels + level), :] = x
+            packed = jnp.where(pair == slot + field, pltpu.roll(x, 2 * (slot + field), 1), packed)
+        return below + term, packed
+
+    packed_mass = pltpu.roll(sum_in_block(mass), 4 * n_fields, 1)
+
+    def one(turn, below):
+        half = levels // 2 - 1 - turn
+        packed = jnp.where(pair == 2 * n_fields, packed_mass, 0.0)
+        below, packed = one_level(2 * half + 1, n_fields, below, packed)
+        below, packed = one_level(2 * half, 0, below, packed)
+        packed_out[tile_of(half), :] = packed
+        return below
+
+    lax.fori_loop(0, levels // 2, one, jnp.zeros((ROWS, LANES), jnp.float32), unroll=3)
+
+
+def tracers_of(firsts, seconds, mass, table, tracer, before, w_out, packed_out):
     tracers, levels = tracer.shape[:2]
     n_fields = 4 + tracers
     pair = pair_of(iota(1))
-    mass = mass_in[...]
     along_rows = derivative_terms(0, time_step * node_weights())
 
     def one(half, _):
@@ -442,7 +468,7 @@
             copy.wait()
         return 0
 
-    lax.fori_loop(0, levels // 2, one, 0)
+    lax.fori_loop(0, levels // 2, one, 0, unroll=3)
     lax.fori_loop(0, levels, finish, 0)
 
 
@@ -476,35 +502,36 @@
     def in_hbm(x):
         return pltpu.with_memory_space_constraint(x, pltpu.HBM)
 
-    inputs = tuple(in_hbm(x) for x in (air, heat, thick, ground, maps, det, jnp.asarray(lane_tables()), tracer))
+    inputs = tuple(in_hbm(x) for x in (air, heat, thick, ground, maps, det, jnp.asarray(lane_tables())))
     params = pltpu.CompilerParams(vmem_limit_bytes=24 * 1024 * 1024)
-    dynamics, packed, share, *for_tracers = pl.pallas_call(
-        lambda *refs: dynamics_kernel(n_share, fields, *refs),
+    share, *rest = pl.pallas_call(
+        lambda *refs: column_kernel(n_share, *refs),
+        out_shape=(
+            f32(n_share, 2 * ROWS, LANES),
+            f32(7, levels, ROWS, LANES),
+            f32(7, ROWS, LANES),
+            jax.ShapeDtypeStruct(inputs[6].shape, inputs[6].dtype),
+        ),
+        in_specs=[ANY] * 7,
+        out_specs=(VMEM,) * 4,
+        scratch_shapes=[pltpu.SemaphoreType.DMA((7,))],
+        compiler_params=params,
+        name="column",
+    )(*inputs)
+    shared = lax.all_to_all(share, COLUMN, 0, 0, tiled=True)
+    dynamics_w, w, packed = pl.pallas_call(
+        fields_kernel,
         out_shape=(
             f32(4 * levels * ROWS, LANES),
+            f32((edge_rows - 4 * levels) * ROWS, LANES),
             f32(count * ROWS, LANES),
-            f32(n_share, 2 * ROWS, LANES),
-            f32(levels, ROWS, LANES),
-            f32(levels, ROWS, LANES),
-            f32(ROWS, LANES),
-            jax.ShapeDtypeStruct(inputs[6].shape, inputs[6].dtype),
-            f32(*tracer.shape),
         ),
-        in_specs=[ANY] * 8,
-        out_specs=(VMEM,) * 8,
-        scratch_shapes=[pltpu.VMEM(x.shape, x.dtype) for x in inputs[:6]] + [pltpu.SemaphoreType.DMA((8,))],
+        in_specs=[VMEM] * 3 + [ANY],
+        out_specs=(VMEM,) * 3,
+        scratch_shapes=[pltpu.VMEM(tracer.shape, jnp.float32), pltpu.SemaphoreType.DMA((1,))],
         compiler_params=params,
-        name="dynamics",
-    )(*inputs)
-    shared = lax.all_to_all(share, COLUMN, 0, 0, tiled=True)
-    w, packed = pl.pallas_call(
-        tracer_kernel,
-        out_shape=(f32((edge_rows - 4 * levels) * ROWS, LANES), f32(count * ROWS, LANES)),
-        in_specs=[VMEM] * 6,
-        out_specs=(VMEM,) * 2,
-        compiler_params=params,
-        name="tracers",
-    )(*for_tracers, packed)
+        name="fields",
+    )(*rest, in_hbm(tracer))
     wind, far, near, packed, bound = pl.pallas_call(
         lambda *refs: carry_kernel(levels, n_lev, *refs),
         out_shape=(
@@ -518,7 +545,7 @@
         out_specs=(VMEM,) * 5,
         compiler_params=params,
         name="carry",
-    )(shared, dynamics, w, packed, maps, det)
+    )(shared, dynamics_w, w, packed, maps, det)
     far = swap_pairs(far, FACE, 1)
     near = swap_pairs(near, FACE, 0)
     plane = lax.all_to_all(bound, PLANE, 0, 0, tiled=True)
@@ -543,7 +570,7 @@
         compiler_params=params,
         name="sum",
     )
-    air_next, heat_next, thick_next, tracer_next = sums(rotations.reshape(-1), flips.reshape(-1), valences.reshape(-1), w, dynamics, wind, far, near, inside, outside)
+    air_next, heat_next, thick_next, tracer_next = sums(rotations.reshape(-1), flips.reshape(-1), valences.reshape(-1), w, dynamics_w, wind, far, near, inside, outside)
     return air_next, heat_next, thick_next, tracer_next, stepping_bounds
 
 

time: 75.6 us -> 74.3 us (0.983)
  waiting for transfers between devices: 15 us -> 13.7 us
    all_to_all x1, waiting for transfers between devices: 3.66 us -> 2.35 us  [on_device(): shared = lax.all_to_all(share, COLUMN, 0, 0, tiled=True)]
  transfers between devices with their start and end apart: 6 -> 6, of which waited for: 2 -> 2; matrix products, arithmetic and copies ran while one was open for 1% -> 1% of each run, Pallas kernels for 4% -> 6%
where the time goes in v2:
time: 74.3 us; the launch traced here: 73.3 us
  starting transfers between devices  47.4 us (64%)
  waiting for transfers between devices  13.7 us (18%)
  Pallas kernels  10.6 us (14%)
  between operations  0.82 us (1%)
    all_to_all x1, starting transfers between devices, on_device(): plane = lax.all_to_all(bound, PLANE, 0, 0, tiled=True)  22 us
    ppermute x4, starting transfers between devices, swap_pairs(): return lax.ppermute(x, axes, pairs + [(j, i) for i, j in pairs])  18.1 us
    all_to_all x1, waiting for transfers between devices, on_device(): plane = lax.all_to_all(bound, PLANE, 0, 0, tiled=True)  11.4 us
    all_to_all x1, starting transfers between devices, on_device(): shared = lax.all_to_all(share, COLUMN, 0, 0, tiled=True)  7.28 us
    pallas_call x1, Pallas kernels, on_device(): pl.pallas_call(fields_kernel, out_shape=(f32(4 * levels * ROWS, LANES), f...  3.61 us
    pallas_call x1, Pallas kernels, on_device(): sums(rotations.reshape(-1), flips.reshape(-1), valences.reshape(-1), w, d...  2.99 us
    pallas_call x1, Pallas kernels, on_device(): pl.pallas_call(lambda *refs: column_kernel(n_share, *refs), out_shape=(f3...  2.36 us
    all_to_all x1, waiting for transfers between devices, on_device(): shared = lax.all_to_all(share, COLUMN, 0, 0, tiled=True)  2.35 us
  transfers between devices with their start and end apart: 6, of which 2 were waited for; matrix products, arithmetic and copies ran while one was open for 1% of the time, Pallas kernels for 6%

profile of v2, /device:TPU:6, one launch (start us, length us, event | category | flops | bytes accessed | tf_op | source)
XLA Modules:
  0.0 73.3 jit_solution(9597875704844741425)
XLA Ops:
  0.6 0.0 copy-start.1
  0.6 0.0 copy-start
  0.7 2.4 %column.1 = (f32[8,16,128]{2,1,0:T(8,128)}, f32[7,18,8,128]{3,2,1,0:T(8,128)S(1)}, f32[7,8,128]{2,1,0:T(8,128)S(1)}, bf16[640,128]{1,0:T(8,128)(2,1)S(1)}) custom-call(f32[2,18,8,128]{3,2,1,0:T(8,128)} %refs_0_.1, f32[18,8,128]{2,1,0:T(8,128)} %refs_1_.1, f32[18,8,128]{2,1,0:T(8,128)} %refs_2_.1, f32[8,128]{1,0:T(8,128)} %refs_3_.1, f32[4,8,128]{2,1,0:T(8,128)} %refs_4_.3, ...), custom_call_target="tpu_custom_call" | custom-call | tf_op jit(solution)/shard_map/column/pallas_call | solution.py:507
  3.0 7.3 %all-to-all-start = ((f32[8,16,128]{2,1,0:T(8,128)}), f32[8,16,128]{2,1,0:T(8,128)S(1)}, u32[]{:S(2)}, u32[]{:S(2)}) async-start(f32[8,16,128]{2,1,0:T(8,128)} %get-tuple-element.26), calls=%async_computation | async-start | bytes 131072 | tf_op jit(solution)/shard_map/all_to_all | solution.py:521
  10.3 3.6 %fields.1 = (f32[576,128]{1,0:T(8,128)S(1)}, f32[2624,128]{1,0:T(8,128)S(1)}, f32[72,128]{1,0:T(8,128)S(1)}) custom-call(f32[7,18,8,128]{3,2,1,0:T(8,128)S(1)} %get-tuple-element.21.by_level, f32[7,8,128]{2,1,0:T(8,128)S(1)} %get-tuple-element.22.by_point, bf16[640,128]{1,0:T(8,128)(2,1)S(1)} %get-tuple-element.23.table, f32[18,18,8,128]{3,2,1,0:T(8,128)} %tracer_in.1), custom_call_target="tpu_custom_call" | custom-call | tf_op jit(solution)/shard_map/fields/pallas_call | solution.py:522
  13.9 0.0 copy-start.4
  13.9 0.0 copy-start.2
  13.9 0.0 copy-start.3
  14.0 2.4 %all-to-all-done.refs_0_ = f32[8,16,128]{2,1,0:T(8,128)S(1)} async-done(((f32[8,16,128]{2,1,0:T(8,128)}), f32[8,16,128]{2,1,0:T(8,128)S(1)}, u32[]{:S(2)}, u32[]{:S(2)}) %all-to-all-start) | async-done | bytes 65568 | tf_op jit(solution)/shard_map/all_to_all | solution.py:521
  16.3 0.0 copy-done.1
  16.3 0.0 copy-done
  16.3 0.9 %carry.1 = (f32[288,128]{1,0:T(8,128)S(1)}, f32[416,128]{1,0:T(8,128)S(1)}, f32[416,128]{1,0:T(8,128)S(1)}, f32[72,128]{1,0:T(8,128)S(1)}, f32[128,1,128]{2,1,0:T(1,128)}) custom-call(f32[8,16,128]{2,1,0:T(8,128)S(1)} %all-to-all-done.refs_0_, f32[576,128]{1,0:T(8,128)S(1)} %get-tuple-element.25.refs_1_.refs_4_, ...), custom_call_target="tpu_custom_call" | custom-call | tf_op jit(solution)/shard_map/carry/pallas_call | solution.py:535
  17.2 10.8 %collective-permute-start = (f32[416,128]{1,0:T(8,128)S(1)}, f32[416,128]{1,0:T(8,128)S(1)}, u32[]{:S(2)}, u32[]{:S(2)}) collective-permute-start(f32[416,128]{1,0:T(8,128)S(1)} %get-tuple-element.29), channel_id=1, source_target_pairs={{64,128},{192,256},{320,384},{448,512},{576,640},{704,768},{832,89... | collective-permute-start | bytes 638984 | tf_op jit(solution)/shard_map/ppermute | solution.py:478
  28.1 1.9 %collective-permute-start.1 = (f32[416,128]{1,0:T(8,128)S(1)}, f32[416,128]{1,0:T(8,128)S(1)}, u32[]{:S(2)}, u32[]{:S(2)}) collective-permute-start(f32[416,128]{1,0:T(8,128)S(1)} %get-tuple-element.30), channel_id=1, source_target_pairs={{0,64},{128,192},{256,320},{384,448},{512,576},{640,704},{768,832}... | collective-permute-start | bytes 638984 | tf_op jit(solution)/shard_map/ppermute | solution.py:478
  30.0 22.0 %all-to-all-start.1 = ((f32[128,1,128]{2,1,0:T(1,128)}), f32[128,1,128]{2,1,0:T(1,128)S(1)}, u32[]{:S(2)}, u32[]{:S(2)}) async-start(f32[128,1,128]{2,1,0:T(1,128)} %get-tuple-element.36), calls=%async_computation.1 | async-start | bytes 131072 | tf_op jit(solution)/shard_map/all_to_all | solution.py:551
  52.0 0.0 collective-permute-done.refs_6_
  52.0 0.0 collective-permute-done.1.refs_7_
  52.1 3.2 %collective-permute-start.3 = (f32[104,128]{1,0:T(8,128)S(1)}, f32[104,128]{1,0:T(8,128)S(1)}, u32[]{:S(2)}, u32[]{:S(2)}) collective-permute-start(f32[104,128]{1,0:T(8,128)S(1)} %pad_maximum_fusion), channel_id=1, source_target_pairs={{4,8},{12,16},{20,24},{28,32},{36,40},{44,48},{52,56},{60,0},{8,4}... | collective-permute-start | bytes 159752 | tf_op jit(solution)/shard_map/ppermute | solution.py:478
  55.3 2.2 %collective-permute-start.2 = (f32[104,128]{1,0:T(8,128)S(1)}, f32[104,128]{1,0:T(8,128)S(1)}, u32[]{:S(2)}, u32[]{:S(2)}) collective-permute-start(f32[104,128]{1,0:T(8,128)S(1)} %pad_maximum_fusion), channel_id=1, source_target_pairs={{0,4},{8,12},{16,20},{24,28},{32,36},{40,44},{48,52},{56,60},{4,0}... | collective-permute-start | bytes 159752 | tf_op jit(solution)/shard_map/ppermute | solution.py:478
  57.5 0.0 copy-done.4
  57.5 0.1 reshape.21.refs_2_
  57.6 0.0 copy-done.2
  57.6 0.2 copy.16
  57.7 0.1 reshape.19.refs_0_
  57.9 0.0 copy-done.3
  57.9 0.2 copy.17
  58.1 0.1 reshape.20.refs_1_
  58.2 11.4 %all-to-all-done.1.plane = f32[128,1,128]{2,1,0:T(1,128)S(1)} async-done(((f32[128,1,128]{2,1,0:T(1,128)}), f32[128,1,128]{2,1,0:T(1,128)S(1)}, u32[]{:S(2)}, u32[]{:S(2)}) %all-to-all-start.1) | async-done | bytes 65568 | tf_op jit(solution)/shard_map/all_to_all | solution.py:551
  69.6 0.7 bounds.1
  70.3 0.0 collective-permute-done.3.refs_9_
  70.3 0.0 collective-permute-done.2.refs_8_
  70.3 3.0 %sum.1 = (f32[2,18,8,128]{3,2,1,0:T(8,128)}, f32[18,8,128]{2,1,0:T(8,128)}, f32[18,8,128]{2,1,0:T(8,128)}, f32[18,18,8,128]{3,2,1,0:T(8,128)}) custom-call(s32[512]{0:T(512)S(1)} %reshape.19.refs_0_, s32[512]{0:T(512)S(1)} %reshape.20.refs_1_, s32[256]{0:T(256)S(1)} %reshape.21.refs_2_, f32[2624,128]{1,0:T(8,128)S(1)} %get-tuple-element.24.refs_2_.refs_3_, ...), custom_call_target="tpu_custom_call" | custom-call | tf_op jit(solution)/shard_map/sum/pallas_call | solution.py:573
  (3 shorter events, 0.0 us)
Async XLA Ops:
  0.6 15.7 %copy-start.1 = (f32[8,128]{1,0:T(8,128)S(1)}, f32[8,128]{1,0:T(8,128)}, u32[]{:S(2)}) copy-start(f32[8,128]{1,0:T(8,128)} %refs_5_.3) | copy-start | bytes 12292
  0.6 15.7 %copy-start = (f32[4,8,128]{2,1,0:T(8,128)S(1)}, f32[4,8,128]{2,1,0:T(8,128)}, u32[]{:S(2)}) copy-start(f32[4,8,128]{2,1,0:T(8,128)} %refs_4_.3) | copy-start | bytes 49156
  3.0 13.3 %all-to-all-start = ((f32[8,16,128]{2,1,0:T(8,128)}), f32[8,16,128]{2,1,0:T(8,128)S(1)}, u32[]{:S(2)}, u32[]{:S(2)}) async-start(f32[8,16,128]{2,1,0:T(8,128)} %get-tuple-element.26), calls=%async_computation | async-start | bytes 131072 | tf_op jit(solution)/shard_map/all_to_all | solution.py:521
  13.9 43.6 %copy-start.4 = (s32[16,16]{1,0:T(8,128)S(1)}, s32[16,16]{1,0:T(8,128)}, u32[]{:S(2)}) copy-start(s32[16,16]{1,0:T(8,128)} %param.20) | copy-start | bytes 3076
  13.9 43.6 %copy-start.2 = (s32[16,16,2]{1,2,0:T(2,128)S(1)}, s32[16,16,2]{1,2,0:T(2,128)}, u32[]{:S(2)}) copy-start(s32[16,16,2]{1,2,0:T(2,128)} %param.18) | copy-start | bytes 6148
  13.9 43.9 %copy-start.3 = (s32[16,16,2]{1,2,0:T(2,128)S(1)}, s32[16,16,2]{1,2,0:T(2,128)}, u32[]{:S(2)}) copy-start(s32[16,16,2]{1,2,0:T(2,128)} %param.19) | copy-start | bytes 6148
  17.2 34.8 %collective-permute-start = (f32[416,128]{1,0:T(8,128)S(1)}, f32[416,128]{1,0:T(8,128)S(1)}, u32[]{:S(2)}, u32[]{:S(2)}) collective-permute-start(f32[416,128]{1,0:T(8,128)S(1)} %get-tuple-element.29), channel_id=1, source_target_pairs={{64,128},{192,256},{320,384},{448,512},{576,640},{704,768},{832,89... | collective-permute-start | bytes 638984 | tf_op jit(solution)/shard_map/ppermute | solution.py:478
  28.1 24.0 %collective-permute-start.1 = (f32[416,128]{1,0:T(8,128)S(1)}, f32[416,128]{1,0:T(8,128)S(1)}, u32[]{:S(2)}, u32[]{:S(2)}) collective-permute-start(f32[416,128]{1,0:T(8,128)S(1)} %get-tuple-element.30), channel_id=1, source_target_pairs={{0,64},{128,192},{256,320},{384,448},{512,576},{640,704},{768,832}... | collective-permute-start | bytes 638984 | tf_op jit(solution)/shard_map/ppermute | solution.py:478
  30.0 39.6 %all-to-all-start.1 = ((f32[128,1,128]{2,1,0:T(1,128)}), f32[128,1,128]{2,1,0:T(1,128)S(1)}, u32[]{:S(2)}, u32[]{:S(2)}) async-start(f32[128,1,128]{2,1,0:T(1,128)} %get-tuple-element.36), calls=%async_computation.1 | async-start | bytes 131072 | tf_op jit(solution)/shard_map/all_to_all | solution.py:551
  52.1 18.2 %collective-permute-start.3 = (f32[104,128]{1,0:T(8,128)S(1)}, f32[104,128]{1,0:T(8,128)S(1)}, u32[]{:S(2)}, u32[]{:S(2)}) collective-permute-start(f32[104,128]{1,0:T(8,128)S(1)} %pad_maximum_fusion), channel_id=1, source_target_pairs={{4,8},{12,16},{20,24},{28,32},{36,40},{44,48},{52,56},{60,0},{8,4}... | collective-permute-start | bytes 159752 | tf_op jit(solution)/shard_map/ppermute | solution.py:478
  55.3 15.0 %collective-permute-start.2 = (f32[104,128]{1,0:T(8,128)S(1)}, f32[104,128]{1,0:T(8,128)S(1)}, u32[]{:S(2)}, u32[]{:S(2)}) collective-permute-start(f32[104,128]{1,0:T(8,128)S(1)} %pad_maximum_fusion), channel_id=1, source_target_pairs={{0,4},{8,12},{16,20},{24,28},{32,36},{40,44},{48,52},{56,60},{4,0}... | collective-permute-start | bytes 159752 | tf_op jit(solution)/shard_map/ppermute | solution.py:478
